TPU v7x, 256 devices: a whole 4x4x8 slice. The times are simulated.
256 devices in a mesh: ep: 128 (over z, x, y), half: 2 (over core).
Axes of the slice: x: 4, y: 4, z: 8, core: 2. Of those that a mesh axis runs over, the one named last changes fastest.
Arguments:
- tokens: bfloat16 [16384, 2048], P('ep', 'half'), may hold values from -6 to 6
- gate_weights: float32 [16384, 8], P('ep'), may hold values from 0.05 to 0.3
- expert_ids: int32 [16384, 8], P('ep'), may hold values from 0 to 127, all different within a row; in each aligned block of 128 rows (0 to 127, 128 to 255, ...) at most 10 rows name the same one
- w_gate: bfloat16 [128, 2048, 768], P('ep', None, 'half'), may hold values from -0.125 to 0.125
- w_up: bfloat16 [128, 2048, 768], P('ep', None, 'half'), may hold values from -0.125 to 0.125
- w_down: bfloat16 [128, 768, 2048], P('ep', 'half'), may hold values from -0.21875 to 0.21875
Outputs:
- mixed: bfloat16 [16384, 2048], P('ep', 'half')
Inputs may be any that keep to these rules, and one draw needn't show every extreme that they name: `expert_ids`: each row names 8 different experts. Within the rows of one device (aligned blocks of 128 rows) no expert is named by more than 10 rows, and in every draw some expert is named by exactly 10 rows of some block.
All inputs are finite; a program needn't handle non-finite values.
Results may differ from a plain program's by a relative error of at most 0.0085.
Values may be sent and summed in bfloat16 or wider, within the bound.
No kernel may reach another device: no remote copies, remote signals or barrier semaphores. Data moves between devices by JAX's collectives and lax.ppermute only.
A program may use at most 64 MiB of HBM per device.

v0:
```python
import functools

import jax
import jax.numpy as jnp
from jax import lax
from jax.experimental import pallas as pl
from jax.experimental.pallas import tpu as pltpu
from jax.sharding import Mesh, PartitionSpec as P


F32 = jnp.float32
BF16 = jnp.bfloat16
CAP = 10
TOK = 128
WIDE = 2048
HALF = 1024
PART = 512
FH = 384
PLANE = 16
SUB = 8
LEFT = WIDE // SUB
PIECES = {0: 5, 1: 10, 2: 10, 3: 10, 4: 5}
CHUNKS = ((0, 1, 2), (3, 4))
EXPERT_VMEM = 56
ROUTE_VMEM = 58


def iota(shape, dim):
    return lax.broadcasted_iota(jnp.int32, shape, dim)


def plan(chunk):
    first = {}
    n = 0
    for d in chunk:
        first[d] = n
        n += PIECES[d]
    left = n % SUB == 1
    tiles = n // SUB if left else -(-n // SUB)
    return tiles, left, first


def lanes_of(chunk):
    tiles, left, _ = plan(chunk)
    return tiles * WIDE + (LEFT if left else 0)


def tiles_of(chunk, d):
    tiles, left, first = plan(chunk)
    at, end = first[d], first[d] + PIECES[d]
    return [j for j in range(tiles) if at < (j + 1) * SUB and end > j * SUB], left and end > tiles * SUB


def route_body(tok_ref, ids_ref, w_ref, a_ref):
    ids = ids_ref[...]
    experts = iota((128, TOK), 0)
    named = jnp.zeros((128, TOK), F32)
    for k in range(8):
        named = jnp.where(ids[k : k + 1, :] == experts, 1.0, named)
    before = jnp.where(iota((TOK, TOK), 0) < iota((TOK, TOK), 1), 1.0, 0.0)
    count = jnp.dot(named.astype(BF16), before.astype(BF16), preferred_element_type=F32)
    ranks = [
        jnp.sum(jnp.where(ids[k : k + 1, :] == experts, count, 0.0), axis=0, keepdims=True)
        for k in range(8)
    ]
    w = w_ref[...]
    hi = w.astype(BF16)
    a_ref[0:TOK, :] = tok_ref[...]
    a_ref[TOK : TOK + 8, 0:128] = ids.astype(F32).astype(BF16)
    a_ref[TOK : TOK + 8, 128:256] = jnp.concatenate(ranks, axis=0).astype(BF16)
    a_ref[TOK : TOK + 8, 256:384] = hi
    a_ref[TOK : TOK + 8, 384:512] = (w - hi.astype(F32)).astype(BF16)
    a_ref[TOK : TOK + 8, 512:1024] = jnp.zeros((8, 512), BF16)


def slot_table(info, first, half, slots, values):
    ids = info[:, 0:128].astype(F32)
    rank = info[:, 128:256].astype(F32)
    mine = iota((PLANE, TOK), 0).astype(F32) + first.astype(F32)
    slot = jnp.full((PLANE, TOK), -1000.0, F32)
    picked = [jnp.zeros((PLANE, TOK), F32) for _ in values]
    for k in range(8):
        hit = ids[k : k + 1, :] == mine
        slot = jnp.where(hit, rank[k : k + 1, :], slot)
        for i, at in enumerate(values):
            value = info[:, at : at + 128].astype(F32)
            picked[i] = jnp.where(hit, value[k : k + 1, :], picked[i])
    slot = slot.astype(jnp.int32)
    if slots < CAP:
        slot = slot - half * slots
        slot = jnp.where((slot >= 0) & (slot < slots), slot, -1000)
    return slot, picked


def placed(row, value=None):
    hit = row[:, None, :] == iota((PLANE, SUB, TOK), 1)
    out = jnp.where(hit, 1.0 if value is None else value[:, None, :], 0.0)
    return out.astype(BF16).reshape(PLANE * SUB, TOK)


def dispatch_body(chunk, scal_ref, *refs):
    number = len(chunk)
    out_ref = refs[2 * number]
    tiles, left, first = plan(chunk)
    slots = {}
    for i, d in enumerate(chunk):
        info = refs[2 * i][TOK : TOK + 8, 0:512]
        refs[2 * number + 1 + i][...] = info
        slot, _ = slot_table(info, scal_ref[0], scal_ref[1], PIECES[d], ())
        slots[d] = slot + first[d]
    for j in range(tiles):
        users = [(i, d) for i, d in enumerate(chunk) if j in tiles_of(chunk, d)[0]]
        onehot = jnp.concatenate([placed(slots[d] - SUB * j) for _, d in users], axis=1)
        for p in range(2):
            rows = jnp.concatenate([refs[2 * i + p][0:TOK, :] for i, _ in users], axis=0)
            at = j * WIDE + p * HALF
            out_ref[:, at : at + HALF] = jnp.dot(onehot, rows, preferred_element_type=F32).astype(BF16)
    if left:
        i = number - 1
        here = slots[chunk[i]] == tiles * SUB
        onehot = jnp.concatenate([placed(jnp.where(here, q, -1)) for q in range(SUB)], axis=1)
        per = HALF // LEFT
        rows = jnp.concatenate(
            [
                refs[2 * i + q // per][0:TOK, q % per * LEFT : (q % per + 1) * LEFT]
                for q in range(SUB)
            ],
            axis=0,
        )
        out_ref[:, tiles * WIDE :] = jnp.dot(onehot, rows, preferred_element_type=F32).astype(BF16)


def expert_body(chunk, scal_ref, x_ref, gm_ref, gp_ref, um_ref, up_ref, dm_ref, dp_ref, out_ref, wm, wp, wd, sems):
    half = scal_ref[1]
    side_width = WIDE // 2
    copies = []
    for side in range(2):
        at = pl.multiple_of((half if side == 0 else 1 - half) * side_width, side_width)
        here = pl.ds(at, side_width)
        to = pl.ds(side * side_width, side_width)
        for i, (src, dst, lane) in enumerate(((gm_ref, wm, 0), (um_ref, wm, FH), (gp_ref, wp, 0), (up_ref, wp, FH))):
            copies.append((i, src.at[here, :], dst.at[to, pl.ds(lane, FH)]))
        for i, (src, row) in enumerate(((dm_ref, 0), (dp_ref, FH))):
            copies.append((4 + i, src.at[:, here], wd.at[pl.ds(row, FH), to]))
    copies.sort(key=lambda c: c[0])
    copies = [pltpu.make_async_copy(src, dst, sems.at[n]) for n, (_, src, dst) in enumerate(copies)]
    for c in copies:
        c.start()
    tiles, left, _ = plan(chunk)
    blocks = [x_ref[:, j * WIDE : (j + 1) * WIDE] for j in range(tiles)]
    if left:
        rows = x_ref[:, tiles * WIDE :]
        apart = iota((PLANE, PLANE * SUB), 1) - SUB * iota((PLANE, PLANE * SUB), 0)
        blocks.append(
            jnp.concatenate(
                [
                    jnp.dot(
                        jnp.where(apart == q, 1.0, 0.0).astype(BF16), rows, preferred_element_type=F32
                    ).astype(BF16)
                    for q in range(SUB)
                ],
                axis=1,
            )
        )
    x = jnp.concatenate(blocks, axis=0)
    hidden = []
    for i, w in enumerate((wm, wp)):
        for c in copies[4 * i : 4 * i + 4]:
            c.wait()
        both = jnp.dot(x, w[...], preferred_element_type=F32)
        gate = both[:, :FH]
        hidden.append((gate / (1.0 + jnp.exp(-gate)) * both[:, FH:]).astype(BF16))
    for c in copies[8:]:
        c.wait()
    y = jnp.dot(jnp.concatenate(hidden, axis=1), wd[...], preferred_element_type=F32).astype(BF16)
    size = PLANE * SUB
    for j in range(tiles):
        out_ref[:, j * WIDE : (j + 1) * WIDE] = y[j * size : (j + 1) * size, :]
    if left:
        apart = iota((size, PLANE), 0) - SUB * iota((size, PLANE), 1)
        total = None
        for q in range(SUB):
            spread = jnp.where(apart == q, 1.0, 0.0).astype(BF16)
            part = jnp.dot(spread, y[tiles * size :, q * LEFT : (q + 1) * LEFT], preferred_element_type=F32)
            total = part if total is None else total + part
        out_ref[:, tiles * WIDE :] = total.astype(BF16)


def combine_body(chunk, d, last, scal_ref, info_ref, *refs):
    tiles, _, first = plan(chunk)
    used, over = tiles_of(chunk, d)
    slot, values = slot_table(info_ref[...], scal_ref[0], scal_ref[1], PIECES[d], (256, 384))
    slot = slot + first[d]
    weights = jnp.concatenate([placed(slot - SUB * j, value) for j in used for value in values], axis=0)
    rows = jnp.concatenate([refs[n][...] for n in range(len(used)) for _ in values], axis=0)
    total = lax.dot_general(weights, rows, (((0,), (0,)), ((), ())), preferred_element_type=F32)
    at = len(used)
    if over:
        here = slot == tiles * SUB
        weights = jnp.concatenate(
            [
                jnp.concatenate([placed(jnp.where(here, q, -1), value) for q in range(SUB)], axis=1)
                for value in values
            ],
            axis=0,
        )
        rows = jnp.concatenate([refs[at][...] for _ in values], axis=0)
        extra = lax.dot_general(weights, rows, (((0,), (0,)), ((), ())), preferred_element_type=F32)
        total = total + jnp.concatenate([extra[q * TOK : (q + 1) * TOK, :] for q in range(SUB)], axis=1)
        at += 1
    parts = [total[:, p * PART : (p + 1) * PART] for p in range(4)]
    if last:
        parts = [part + refs[at + p][...].astype(F32) for p, part in enumerate(parts)]
        for side in range(2):
            out = refs[at + 4 + side]
            out[...] = jnp.concatenate(parts[2 * side : 2 * side + 2], axis=1).astype(out.dtype)
    else:
        for p in range(4):
            out = refs[at + p]
            out[...] = parts[p].astype(out.dtype)


def whole(shape):
    return pl.BlockSpec(shape, lambda i: (0,) * len(shape))


def lane_block(shape, at):
    return pl.BlockSpec(shape, lambda i: (0, at))


SMEM = pl.BlockSpec(memory_space=pltpu.SMEM)
HBM = pl.BlockSpec(memory_space=pltpu.HBM)


def kernel(body, out, in_specs, scratch=(), vmem=16):
    return pl.pallas_call(
        body,
        out_shape=[jax.ShapeDtypeStruct(*o) for o in out],
        grid=(1,),
        in_specs=in_specs,
        out_specs=[whole(o[0]) for o in out],
        scratch_shapes=list(scratch),
        compiler_params=pltpu.CompilerParams(vmem_limit_bytes=vmem * 1024 * 1024),
    )


def staged(tokens, gate_weights, expert_ids, w_gate, w_up, w_down):
    z = lax.axis_index("z")
    half = lax.axis_index("half")
    zs = lax.axis_size("z")
    scal = jnp.stack([z * PLANE, half]).astype(jnp.int32)
    swap = [(0, 1), (1, 0)]
    forth = []
    for i in range(zs):
        forth.append((i * 2, (i + 1) % zs * 2))
        forth.append((i * 2 + 1, (i - 1) % zs * 2 + 1))
    back = [(b, a) for a, b in forth]
    size = PLANE * SUB

    side = (TOK, HALF)
    other = lax.ppermute(tokens, "half", swap)
    (own,) = kernel(
        route_body, [((TOK + 8, HALF), BF16)], [whole(side), whole((8, TOK)), whole((8, TOK))], vmem=ROUTE_VMEM
    )(tokens, expert_ids.T, gate_weights.T)
    held = {0: [own, other]}
    for d in range(1, 5):
        held[d] = [lax.ppermute(v, ("z", "half"), forth) for v in held[d - 1]]
    mine = (w_gate[0], w_up[0], w_down[0])
    gated = lax.optimization_barrier((other,) + mine)
    theirs = [lax.ppermute(w, "half", swap) for w in gated[1:]]

    answers = {}
    for chunk in CHUNKS:
        lanes = lanes_of(chunk)
        arrays = [v for d in chunk for v in held[d]]
        sent, *infos = kernel(
            functools.partial(dispatch_body, chunk),
            [((size, lanes), BF16)] + [((8, 512), BF16) for _ in chunk],
            [SMEM] + [whole(v.shape) for v in arrays],
        )(scal, *arrays)
        got = lax.all_to_all(sent.reshape(PLANE, SUB, lanes), ("x", "y"), 0, 0, tiled=True)
        (result,) = kernel(
            functools.partial(expert_body, chunk),
            [((size, lanes), BF16)],
            [SMEM, whole((size, lanes))] + [HBM] * 6,
            (
                pltpu.VMEM((WIDE, 2 * FH), BF16),
                pltpu.VMEM((WIDE, 2 * FH), BF16),
                pltpu.VMEM((2 * FH, WIDE), BF16),
                pltpu.SemaphoreType.DMA((12,)),
            ),
            EXPERT_VMEM,
        )(scal, got.reshape(size, lanes), mine[0], theirs[0], mine[1], theirs[1], mine[2], theirs[2])
        returned = lax.all_to_all(result.reshape(PLANE, SUB, lanes), ("x", "y"), 0, 0, tiled=True)
        for d, info in zip(chunk, infos):
            answers[d] = (chunk, returned.reshape(size, lanes), info)

    received = []
    for d in (4, 3, 2, 1, 0):
        chunk, value, info = answers[d]
        used, over = tiles_of(chunk, d)
        specs = [lane_block((size, WIDE), j) for j in used]
        if over:
            specs.append(lane_block((size, LEFT), plan(chunk)[0] * SUB))
        last = d == 0
        extra = received if last else []
        outs = kernel(
            functools.partial(combine_body, chunk, d, last),
            [(side, F32), (side, BF16)] if last else [((TOK, PART), F32 if received else BF16)] * 4,
            [SMEM, whole((8, 512))] + specs + [whole((TOK, PART)) for _ in extra],
        )(scal, info, *[value for _ in specs], *extra)
        if not last:
            if received:
                outs = [(v + r.astype(F32)).astype(BF16) for v, r in zip(outs, received)]
            received = [lax.ppermute(v, ("z", "half"), back) for v in outs]
    kept, given = outs
    return (kept + lax.ppermute(given, "half", swap).astype(F32)).astype(BF16)


def solution(mesh):
    spaced = Mesh(mesh.devices.reshape(8, 4, 4, 2), ("z", "x", "y", "half"))
    ep = ("z", "x", "y")
    specs = (
        P(ep, "half"),
        P(ep, None),
        P(ep, None),
        P(ep, None, "half"),
        P(ep, None, "half"),
        P(ep, "half", None),
    )
    return jax.shard_map(staged, mesh=spaced, in_specs=specs, out_specs=P(ep, "half"), check_vma=False)
```

profile of v0, /device:TPU:1, one launch (start us, length us, event | category | flops | bytes accessed | tf_op | source)
XLA Modules:
  0.0 155.4 jit_solution(3542573668028054572)
XLA Ops:
  0.0 3.2 %collective-permute-start = (bf16[128,1024]{1,0:T(8,128)(2,1)}, bf16[128,1024]{1,0:T(8,128)(2,1)S(1)}, u32[]{:S(2)}, u32[]{:S(2)}) collective-permute-start(bf16[128,1024]{1,0:T(8,128)(2,1)} %tok_ref.1), channel_id=1, source_target_pairs={{0,1},{1,0},{2,3},{3,2},{4,5},{5,4},{6,7},{7,6},{8,9},{9,8},{10,11... | collective-permute-start | bytes 786440 | tf_op jit(solution)/shard_map/ppermute | solution.py:261
  3.2 1.9 %shard_map.64.refs_0_ = bf16[136,1024]{1,0:T(8,128)(2,1)} custom-call(bf16[128,1024]{1,0:T(8,128)(2,1)} %tok_ref.1, s32[8,128]{1,0:T(8,128)} %bitcast.37, f32[8,128]{1,0:T(8,128)} %bitcast.38), custom_call_target="tpu_custom_call" | custom-call | tf_op jit(solution)/shard_map/pallas_call | solution.py:262
  5.1 3.9 %collective-permute-start.1 = (bf16[136,1024]{1,0:T(8,128)(2,1)}, bf16[136,1024]{1,0:T(8,128)(2,1)S(1)}, u32[]{:S(2)}, u32[]{:S(2)}) collective-permute-start(bf16[136,1024]{1,0:T(8,128)(2,1)} %shard_map.64.refs_0_), channel_id=1, source_target_pairs={{0,32},{1,225},{32,64},{33,1},{64,96},{65,33},{96,128},{97,65},{12... | collective-permute-start | bytes 835592 | tf_op jit(solution)/shard_map/ppermute | solution.py:267
  9.0 0.7 collective-permute-start.2
  9.7 3.1 %collective-permute-done.1.refs_2_ = bf16[136,1024]{1,0:T(8,128)(2,1)S(1)} collective-permute-done((bf16[136,1024]{1,0:T(8,128)(2,1)}, bf16[136,1024]{1,0:T(8,128)(2,1)S(1)}, u32[]{:S(2)}, u32[]{:S(2)}) %collective-permute-start.1) | collective-permute-done | bytes 278560 | tf_op jit(solution)/shard_map/ppermute | solution.py:267
  12.8 3.0 %collective-permute-start.3 = (bf16[136,1024]{1,0:T(8,128)(2,1)S(1)}, bf16[136,1024]{1,0:T(8,128)(2,1)S(1)}, u32[]{:S(2)}, u32[]{:S(2)}) collective-permute-start(bf16[136,1024]{1,0:T(8,128)(2,1)S(1)} %collective-permute-done.1.refs_2_), channel_id=1, source_target_pairs={{0,32},{1,225},{32,64},{33,1},{64,96},{65,33},{96,128},{97,65},{12... | collective-permute-start | bytes 835592 | tf_op jit(solution)/shard_map/ppermute | solution.py:267
  15.8 2.8 %collective-permute-start.4 = (bf16[128,1024]{1,0:T(8,128)(2,1)S(1)}, bf16[128,1024]{1,0:T(8,128)(2,1)S(1)}, u32[]{:S(2)}, u32[]{:S(2)}) collective-permute-start(bf16[128,1024]{1,0:T(8,128)(2,1)S(1)} %collective-permute-done.2.refs_3_), channel_id=1, source_target_pairs={{0,32},{1,225},{32,64},{33,1},{64,96},{65,33},{96,128},{97,65},{12... | collective-permute-start | bytes 786440 | tf_op jit(solution)/shard_map/ppermute | solution.py:267
  18.6 0.7 collective-permute-done.3.refs_4_
  19.3 3.1 %collective-permute-start.8 = (bf16[136,1024]{1,0:T(8,128)(2,1)S(1)}, bf16[136,1024]{1,0:T(8,128)(2,1)S(1)}, u32[]{:S(2)}, u32[]{:S(2)}) collective-permute-start(bf16[136,1024]{1,0:T(8,128)(2,1)S(1)} %collective-permute-done.3.refs_4_), channel_id=1, source_target_pairs={{0,32},{1,225},{32,64},{33,1},{64,96},{65,33},{96,128},{97,65},{12... | collective-permute-start | bytes 835592 | tf_op jit(solution)/shard_map/ppermute | solution.py:267
  22.4 2.8 %collective-permute-start.9 = (bf16[128,1024]{1,0:T(8,128)(2,1)S(1)}, bf16[128,1024]{1,0:T(8,128)(2,1)S(1)}, u32[]{:S(2)}, u32[]{:S(2)}) collective-permute-start(bf16[128,1024]{1,0:T(8,128)(2,1)S(1)} %collective-permute-done.4.refs_5_), channel_id=1, source_target_pairs={{0,32},{1,225},{32,64},{33,1},{64,96},{65,33},{96,128},{97,65},{12... | collective-permute-start | bytes 786440 | tf_op jit(solution)/shard_map/ppermute | solution.py:267
  25.2 0.7 collective-permute-done.8.refs_0_
  25.9 3.1 %collective-permute-start.10 = (bf16[136,1024]{1,0:T(8,128)(2,1)S(1)}, bf16[136,1024]{1,0:T(8,128)(2,1)S(1)}, u32[]{:S(2)}, u32[]{:S(2)}) collective-permute-start(bf16[136,1024]{1,0:T(8,128)(2,1)S(1)} %collective-permute-done.8.refs_0_), channel_id=1, source_target_pairs={{0,32},{1,225},{32,64},{33,1},{64,96},{65,33},{96,128},{97,65},{12... | collective-permute-start | bytes 835592 | tf_op jit(solution)/shard_map/ppermute | solution.py:267
  29.0 2.8 %collective-permute-start.11 = (bf16[128,1024]{1,0:T(8,128)(2,1)S(1)}, bf16[128,1024]{1,0:T(8,128)(2,1)S(1)}, u32[]{:S(2)}, u32[]{:S(2)}) collective-permute-start(bf16[128,1024]{1,0:T(8,128)(2,1)S(1)} %collective-permute-done.9.refs_1_), channel_id=1, source_target_pairs={{0,32},{1,225},{32,64},{33,1},{64,96},{65,33},{96,128},{97,65},{12... | collective-permute-start | bytes 786440 | tf_op jit(solution)/shard_map/ppermute | solution.py:267
  31.9 0.6 collective-permute-done.10.refs_2_
  32.5 2.8 %collective-permute-done.11.refs_3_ = bf16[128,1024]{1,0:T(8,128)(2,1)S(1)} collective-permute-done((bf16[128,1024]{1,0:T(8,128)(2,1)S(1)}, bf16[128,1024]{1,0:T(8,128)(2,1)S(1)}, u32[]{:S(2)}, u32[]{:S(2)}) %collective-permute-start.11) | collective-permute-done | bytes 262176 | tf_op jit(solution)/shard_map/ppermute | solution.py:267
  35.3 1.9 %shard_map.69 = (bf16[128,4096]{1,0:T(8,128)(2,1)}, bf16[8,512]{1,0:T(8,128)(2,1)S(1)}, bf16[8,512]{1,0:T(8,128)(2,1)S(1)}) custom-call(s32[2]{0:T(128)S(1)} %pad_add_fusion.scal_ref, bf16[136,1024]{1,0:T(8,128)(2,1)S(1)} %collective-permute-done.8.refs_0_, bf16[128,1024]{1,0:T(8,128)(2,1)S(1)} %collective-permute-done.9.refs_1_, ...), custom_call_target="tpu_custom_call" | custom-call | tf_op jit(solution)/shard_map/pallas_call | solution.py:276
  37.3 6.8 %all-to-all-start.2 = ((bf16[16,8,4096]{2,1,0:T(8,128)(2,1)}), bf16[16,8,4096]{2,1,0:T(8,128)(2,1)S(1)}, u32[]{:S(2)}, u32[]{:S(2)}) async-start(bf16[16,8,4096]{2,1,0:T(8,128)(2,1)} %bitcast.11), calls=%async_computation.2 | async-start | bytes 2097152 | tf_op jit(solution)/shard_map/all_to_all | solution.py:281
  44.0 5.1 %collective-permute-start.5 = (bf16[2048,384]{1,0:T(8,128)(2,1)}, bf16[2048,384]{1,0:T(8,128)(2,1)}, u32[]{:S(2)}, u32[]{:S(2)}) collective-permute-start(bf16[2048,384]{1,0:T(8,128)(2,1)} %bitcast.26), channel_id=1, source_target_pairs={{0,1},{1,0},{2,3},{3,2},{4,5},{5,4},{6,7},{7,6},{8,9},{9,8},{10,11... | collective-permute-start | bytes 4718600 | tf_op jit(solution)/shard_map/ppermute | solution.py:270
  49.7 2.4 %shard_map.65 = (bf16[128,6400]{1,0:T(8,128)(2,1)}, bf16[8,512]{1,0:T(8,128)(2,1)S(1)}, bf16[8,512]{1,0:T(8,128)(2,1)S(1)}, bf16[8,512]{1,0:T(8,128)(2,1)S(1)}) custom-call(s32[2]{0:T(128)S(1)} %pad_add_fusion.scal_ref, bf16[136,1024]{1,0:T(8,128)(2,1)S(1)} %copy-done, bf16[128,1024]{1,0:T(8,128)(2,1)S(1)} %collective-permute-done.refs_1_, ...), custom_call_target="tpu_custom_call" | custom-call | tf_op jit(solution)/shard_map/pallas_call | solution.py:276
  52.1 3.8 %all-to-all-done.2 = bf16[16,8,4096]{2,1,0:T(8,128)(2,1)S(1)} async-done(((bf16[16,8,4096]{2,1,0:T(8,128)(2,1)}), bf16[16,8,4096]{2,1,0:T(8,128)(2,1)S(1)}, u32[]{:S(2)}, u32[]{:S(2)}) %all-to-all-start.2) | async-done | bytes 1048608 | tf_op jit(solution)/shard_map/all_to_all | solution.py:281
  55.9 1.0 copy-done.4
  56.8 3.9 %all-to-all-start = ((bf16[16,8,6400]{2,1,0:T(8,128)(2,1)}), bf16[16,8,6400]{2,1,0:T(8,128)(2,1)S(1)}, u32[]{:S(2)}, u32[]{:S(2)}) async-start(bf16[16,8,6400]{2,1,0:T(8,128)(2,1)} %bitcast.4), calls=%async_computation | async-start | bytes 3276800 | tf_op jit(solution)/shard_map/all_to_all | solution.py:281
  60.8 7.7 %shard_map.70 = bf16[128,4096]{1,0:T(8,128)(2,1)} custom-call(s32[2]{0:T(128)} %copy-done.1, bf16[128,4096]{1,0:T(8,128)(2,1)} %bitcast.35, bf16[2048,384]{1,0:T(8,128)(2,1)} %bitcast.27, bf16[2048,384]{1,0:T(8,128)(2,1)} %collective-permute-done.5.gp_ref, bf16[2048,384]{1,0:T(8,128)(2,1)} %bitcast.30, bf16[2048,384]{1,0:T(8,128)(2,1)} %collective-permute-done.6.up_ref, ...), custom_call_target="tpu_custom_call" | custom-call | tf_op jit(solution)/shard_map/pallas_call | solution.py:282
  68.5 8.2 %all-to-all-done = bf16[16,8,6400]{2,1,0:T(8,128)(2,1)S(1)} async-done(((bf16[16,8,6400]{2,1,0:T(8,128)(2,1)}), bf16[16,8,6400]{2,1,0:T(8,128)(2,1)S(1)}, u32[]{:S(2)}, u32[]{:S(2)}) %all-to-all-start) | async-done | bytes 1638432 | tf_op jit(solution)/shard_map/all_to_all | solution.py:281
  76.7 5.7 %all-to-all-start.3 = ((bf16[16,8,4096]{2,1,0:T(8,128)(2,1)}), bf16[16,8,4096]{2,1,0:T(8,128)(2,1)S(1)}, u32[]{:S(2)}, u32[]{:S(2)}) async-start(bf16[16,8,4096]{2,1,0:T(8,128)(2,1)} %bitcast.36), calls=%async_computation.3 | async-start | bytes 2097152 | tf_op jit(solution)/shard_map/all_to_all | solution.py:294
  82.4 9.9 %shard_map.66 = bf16[128,6400]{1,0:T(8,128)(2,1)} custom-call(s32[2]{0:T(128)} %copy-done.1, bf16[128,6400]{1,0:T(8,128)(2,1)} %bitcast.25, bf16[2048,384]{1,0:T(8,128)(2,1)} %bitcast.28, bf16[2048,384]{1,0:T(8,128)(2,1)} %collective-permute-done.5.gp_ref, bf16[2048,384]{1,0:T(8,128)(2,1)} %bitcast.31, bf16[2048,384]{1,0:T(8,128)(2,1)} %collective-permute-done.6.up_ref, ...), custom_call_target="tpu_custom_call" | custom-call | tf_op jit(solution)/shard_map/pallas_call | solution.py:282
  92.3 1.9 %all-to-all-done.3 = bf16[16,8,4096]{2,1,0:T(8,128)(2,1)S(1)} async-done(((bf16[16,8,4096]{2,1,0:T(8,128)(2,1)}), bf16[16,8,4096]{2,1,0:T(8,128)(2,1)S(1)}, u32[]{:S(2)}, u32[]{:S(2)}) %all-to-all-start.3) | async-done | bytes 1048608 | tf_op jit(solution)/shard_map/all_to_all | solution.py:294
  94.2 4.7 %all-to-all-start.1 = ((bf16[16,8,6400]{2,1,0:T(8,128)(2,1)}), bf16[16,8,6400]{2,1,0:T(8,128)(2,1)S(1)}, u32[]{:S(2)}, u32[]{:S(2)}) async-start(bf16[16,8,6400]{2,1,0:T(8,128)(2,1)} %bitcast.24), calls=%async_computation.1 | async-start | bytes 3276800 | tf_op jit(solution)/shard_map/all_to_all | solution.py:294
  99.0 0.9 shard_map.72
  100.0 1.0 shard_map.71
  101.0 7.3 %collective-permute-start.16 = (bf16[128,512]{1,0:T(8,128)(2,1)S(1)}, bf16[128,512]{1,0:T(8,128)(2,1)S(1)}, u32[]{:S(2)}, u32[]{:S(2)}) collective-permute-start(bf16[128,512]{1,0:T(8,128)(2,1)S(1)} %get-tuple-element.50), channel_id=1, source_target_pairs={{32,0},{225,1},{64,32},{1,33},{96,64},{33,65},{128,96},{65,97},{16... | collective-permute-start | bytes 393224 | tf_op jit(solution)/shard_map/ppermute | solution.py:315
  108.3 2.8 %collective-permute-start.20 = (bf16[128,512]{1,0:T(8,128)(2,1)S(1)}, bf16[128,512]{1,0:T(8,128)(2,1)S(1)}, u32[]{:S(2)}, u32[]{:S(2)}) collective-permute-start(bf16[128,512]{1,0:T(8,128)(2,1)S(1)} %get-tuple-element.54), channel_id=1, source_target_pairs={{32,0},{225,1},{64,32},{1,33},{96,64},{33,65},{128,96},{65,97},{16... | collective-permute-start | bytes 393224 | tf_op jit(solution)/shard_map/ppermute | solution.py:315
  111.3 1.6 %collective-permute-done.12 = bf16[128,512]{1,0:T(8,128)(2,1)S(1)} collective-permute-done((bf16[128,512]{1,0:T(8,128)(2,1)S(1)}, bf16[128,512]{1,0:T(8,128)(2,1)S(1)}, u32[]{:S(2)}, u32[]{:S(2)}) %collective-permute-start.12) | collective-permute-done | bytes 131104 | tf_op jit(solution)/shard_map/ppermute | solution.py:315
  113.0 1.3 collective-permute-done.16
  114.3 3.3 %collective-permute-start.17 = (bf16[128,512]{1,0:T(8,128)(2,1)S(1)}, bf16[128,512]{1,0:T(8,128)(2,1)S(1)}, u32[]{:S(2)}, u32[]{:S(2)}) collective-permute-start(bf16[128,512]{1,0:T(8,128)(2,1)S(1)} %add_convert_fusion.9), channel_id=1, source_target_pairs={{32,0},{225,1},{64,32},{1,33},{96,64},{33,65},{128,96},{65,97},{16... | collective-permute-start | bytes 393224 | tf_op jit(solution)/shard_map/ppermute | solution.py:315
  118.2 1.2 shard_map.68
  119.9 1.6 %collective-permute-start.18 = (bf16[128,512]{1,0:T(8,128)(2,1)S(1)}, bf16[128,512]{1,0:T(8,128)(2,1)S(1)}, u32[]{:S(2)}, u32[]{:S(2)}) collective-permute-start(bf16[128,512]{1,0:T(8,128)(2,1)S(1)} %add_convert_fusion.8), channel_id=1, source_target_pairs={{32,0},{225,1},{64,32},{1,33},{96,64},{33,65},{128,96},{65,97},{16... | collective-permute-start | bytes 393224 | tf_op jit(solution)/shard_map/ppermute | solution.py:315
  121.6 4.7 %collective-permute-start.14 = (bf16[128,512]{1,0:T(8,128)(2,1)S(1)}, bf16[128,512]{1,0:T(8,128)(2,1)S(1)}, u32[]{:S(2)}, u32[]{:S(2)}) collective-permute-start(bf16[128,512]{1,0:T(8,128)(2,1)S(1)} %add_convert_fusion.11), channel_id=1, source_target_pairs={{32,0},{225,1},{64,32},{1,33},{96,64},{33,65},{128,96},{65,97},{16... | collective-permute-start | bytes 393224 | tf_op jit(solution)/shard_map/ppermute | solution.py:315
  126.3 5.1 %collective-permute-start.22 = (bf16[128,512]{1,0:T(8,128)(2,1)S(1)}, bf16[128,512]{1,0:T(8,128)(2,1)S(1)}, u32[]{:S(2)}, u32[]{:S(2)}) collective-permute-start(bf16[128,512]{1,0:T(8,128)(2,1)S(1)} %add_convert_fusion.5), channel_id=1, source_target_pairs={{32,0},{225,1},{64,32},{1,33},{96,64},{33,65},{128,96},{65,97},{16... | collective-permute-start | bytes 393224 | tf_op jit(solution)/shard_map/ppermute | solution.py:315
  131.6 1.0 shard_map.67
  132.8 6.5 %collective-permute-start.15 = (bf16[128,512]{1,0:T(8,128)(2,1)S(1)}, bf16[128,512]{1,0:T(8,128)(2,1)S(1)}, u32[]{:S(2)}, u32[]{:S(2)}) collective-permute-start(bf16[128,512]{1,0:T(8,128)(2,1)S(1)} %add_convert_fusion.10), channel_id=1, source_target_pairs={{32,0},{225,1},{64,32},{1,33},{96,64},{33,65},{128,96},{65,97},{16... | collective-permute-start | bytes 393224 | tf_op jit(solution)/shard_map/ppermute | solution.py:315
  139.5 1.7 %collective-permute-done.15.refs_1_ = bf16[128,512]{1,0:T(8,128)(2,1)S(1)} collective-permute-done((bf16[128,512]{1,0:T(8,128)(2,1)S(1)}, bf16[128,512]{1,0:T(8,128)(2,1)S(1)}, u32[]{:S(2)}, u32[]{:S(2)}) %collective-permute-start.15) | collective-permute-done | bytes 131104 | tf_op jit(solution)/shard_map/ppermute | solution.py:315
  141.2 3.2 %collective-permute-done.23.refs_3_ = bf16[128,512]{1,0:T(8,128)(2,1)S(1)} collective-permute-done((bf16[128,512]{1,0:T(8,128)(2,1)S(1)}, bf16[128,512]{1,0:T(8,128)(2,1)S(1)}, u32[]{:S(2)}, u32[]{:S(2)}) %collective-permute-start.23) | collective-permute-done | bytes 131104 | tf_op jit(solution)/shard_map/ppermute | solution.py:315
  144.4 1.4 collective-permute-done.27.refs_4_
  145.8 0.9 shard_map.73
  146.7 6.7 %collective-permute-start.28 = (bf16[128,1024]{1,0:T(8,128)(2,1)S(1)}, bf16[128,1024]{1,0:T(8,128)(2,1)S(1)}, u32[]{:S(2)}, u32[]{:S(2)}) collective-permute-start(bf16[128,1024]{1,0:T(8,128)(2,1)S(1)} %get-tuple-element.60), channel_id=1, source_target_pairs={{0,1},{1,0},{2,3},{3,2},{4,5},{5,4},{6,7},{7,6},{8,9},{9,8},{10,11... | collective-permute-start | bytes 786440 | tf_op jit(solution)/shard_map/ppermute | solution.py:317
  153.4 1.2 collective-permute-done.28
  154.6 0.8 add_convert_fusion
  (52 shorter events, 2.7 us)
Async XLA Ops:
  0.0 9.0 %collective-permute-start = (bf16[128,1024]{1,0:T(8,128)(2,1)}, bf16[128,1024]{1,0:T(8,128)(2,1)S(1)}, u32[]{:S(2)}, u32[]{:S(2)}) collective-permute-start(bf16[128,1024]{1,0:T(8,128)(2,1)} %tok_ref.1), channel_id=1, source_target_pairs={{0,1},{1,0},{2,3},{3,2},{4,5},{5,4},{6,7},{7,6},{8,9},{9,8},{10,11... | collective-permute-start | bytes 786440 | tf_op jit(solution)/shard_map/ppermute | solution.py:261
  5.1 7.7 %collective-permute-start.1 = (bf16[136,1024]{1,0:T(8,128)(2,1)}, bf16[136,1024]{1,0:T(8,128)(2,1)S(1)}, u32[]{:S(2)}, u32[]{:S(2)}) collective-permute-start(bf16[136,1024]{1,0:T(8,128)(2,1)} %shard_map.64.refs_0_), channel_id=1, source_target_pairs={{0,32},{1,225},{32,64},{33,1},{64,96},{65,33},{96,128},{97,65},{12... | collective-permute-start | bytes 835592 | tf_op jit(solution)/shard_map/ppermute | solution.py:267
  9.0 6.8 %collective-permute-start.2 = (bf16[128,1024]{1,0:T(8,128)(2,1)S(1)}, bf16[128,1024]{1,0:T(8,128)(2,1)S(1)}, u32[]{:S(2)}, u32[]{:S(2)}) collective-permute-start(bf16[128,1024]{1,0:T(8,128)(2,1)S(1)} %collective-permute-done.refs_1_), channel_id=1, source_target_pairs={{0,32},{1,225},{32,64},{33,1},{64,96},{65,33},{96,128},{97,65},{12... | collective-permute-start | bytes 786440 | tf_op jit(solution)/shard_map/ppermute | solution.py:267
  12.8 6.5 %collective-permute-start.3 = (bf16[136,1024]{1,0:T(8,128)(2,1)S(1)}, bf16[136,1024]{1,0:T(8,128)(2,1)S(1)}, u32[]{:S(2)}, u32[]{:S(2)}) collective-permute-start(bf16[136,1024]{1,0:T(8,128)(2,1)S(1)} %collective-permute-done.1.refs_2_), channel_id=1, source_target_pairs={{0,32},{1,225},{32,64},{33,1},{64,96},{65,33},{96,128},{97,65},{12... | collective-permute-start | bytes 835592 | tf_op jit(solution)/shard_map/ppermute | solution.py:267
  15.8 6.6 %collective-permute-start.4 = (bf16[128,1024]{1,0:T(8,128)(2,1)S(1)}, bf16[128,1024]{1,0:T(8,128)(2,1)S(1)}, u32[]{:S(2)}, u32[]{:S(2)}) collective-permute-start(bf16[128,1024]{1,0:T(8,128)(2,1)S(1)} %collective-permute-done.2.refs_3_), channel_id=1, source_target_pairs={{0,32},{1,225},{32,64},{33,1},{64,96},{65,33},{96,128},{97,65},{12... | collective-permute-start | bytes 786440 | tf_op jit(solution)/shard_map/ppermute | solution.py:267
  19.3 6.6 %collective-permute-start.8 = (bf16[136,1024]{1,0:T(8,128)(2,1)S(1)}, bf16[136,1024]{1,0:T(8,128)(2,1)S(1)}, u32[]{:S(2)}, u32[]{:S(2)}) collective-permute-start(bf16[136,1024]{1,0:T(8,128)(2,1)S(1)} %collective-permute-done.3.refs_4_), channel_id=1, source_target_pairs={{0,32},{1,225},{32,64},{33,1},{64,96},{65,33},{96,128},{97,65},{12... | collective-permute-start | bytes 835592 | tf_op jit(solution)/shard_map/ppermute | solution.py:267
  22.4 6.6 %collective-permute-start.9 = (bf16[128,1024]{1,0:T(8,128)(2,1)S(1)}, bf16[128,1024]{1,0:T(8,128)(2,1)S(1)}, u32[]{:S(2)}, u32[]{:S(2)}) collective-permute-start(bf16[128,1024]{1,0:T(8,128)(2,1)S(1)} %collective-permute-done.4.refs_5_), channel_id=1, source_target_pairs={{0,32},{1,225},{32,64},{33,1},{64,96},{65,33},{96,128},{97,65},{12... | collective-permute-start | bytes 786440 | tf_op jit(solution)/shard_map/ppermute | solution.py:267
  25.9 6.6 %collective-permute-start.10 = (bf16[136,1024]{1,0:T(8,128)(2,1)S(1)}, bf16[136,1024]{1,0:T(8,128)(2,1)S(1)}, u32[]{:S(2)}, u32[]{:S(2)}) collective-permute-start(bf16[136,1024]{1,0:T(8,128)(2,1)S(1)} %collective-permute-done.8.refs_0_), channel_id=1, source_target_pairs={{0,32},{1,225},{32,64},{33,1},{64,96},{65,33},{96,128},{97,65},{12... | collective-permute-start | bytes 835592 | tf_op jit(solution)/shard_map/ppermute | solution.py:267
  29.0 6.3 %collective-permute-start.11 = (bf16[128,1024]{1,0:T(8,128)(2,1)S(1)}, bf16[128,1024]{1,0:T(8,128)(2,1)S(1)}, u32[]{:S(2)}, u32[]{:S(2)}) collective-permute-start(bf16[128,1024]{1,0:T(8,128)(2,1)S(1)} %collective-permute-done.9.refs_1_), channel_id=1, source_target_pairs={{0,32},{1,225},{32,64},{33,1},{64,96},{65,33},{96,128},{97,65},{12... | collective-permute-start | bytes 786440 | tf_op jit(solution)/shard_map/ppermute | solution.py:267
  31.9 17.8 %copy-start.1 = (s32[2]{0:T(128)}, s32[2]{0:T(128)S(1)}, u32[]{:S(2)}) copy-start(s32[2]{0:T(128)S(1)} %pad_add_fusion.scal_ref) | copy-start | bytes 28
  31.9 17.8 %copy-start = (bf16[136,1024]{1,0:T(8,128)(2,1)S(1)}, bf16[136,1024]{1,0:T(8,128)(2,1)}, u32[]{:S(2)}) copy-start(bf16[136,1024]{1,0:T(8,128)(2,1)} %shard_map.64.refs_0_) | copy-start | bytes 835588
  37.3 18.6 %all-to-all-start.2 = ((bf16[16,8,4096]{2,1,0:T(8,128)(2,1)}), bf16[16,8,4096]{2,1,0:T(8,128)(2,1)S(1)}, u32[]{:S(2)}, u32[]{:S(2)}) async-start(bf16[16,8,4096]{2,1,0:T(8,128)(2,1)} %bitcast.11), calls=%async_computation.2 | async-start | bytes 2097152 | tf_op jit(solution)/shard_map/all_to_all | solution.py:281
  44.0 16.7 %collective-permute-start.5 = (bf16[2048,384]{1,0:T(8,128)(2,1)}, bf16[2048,384]{1,0:T(8,128)(2,1)}, u32[]{:S(2)}, u32[]{:S(2)}) collective-permute-start(bf16[2048,384]{1,0:T(8,128)(2,1)} %bitcast.26), channel_id=1, source_target_pairs={{0,1},{1,0},{2,3},{3,2},{4,5},{5,4},{6,7},{7,6},{8,9},{9,8},{10,11... | collective-permute-start | bytes 4718600 | tf_op jit(solution)/shard_map/ppermute | solution.py:270
  49.2 11.6 %collective-permute-start.6 = (bf16[2048,384]{1,0:T(8,128)(2,1)}, bf16[2048,384]{1,0:T(8,128)(2,1)}, u32[]{:S(2)}, u32[]{:S(2)}) collective-permute-start(bf16[2048,384]{1,0:T(8,128)(2,1)} %bitcast.29), channel_id=1, source_target_pairs={{0,1},{1,0},{2,3},{3,2},{4,5},{5,4},{6,7},{7,6},{8,9},{9,8},{10,11... | collective-permute-start | bytes 4718600 | tf_op jit(solution)/shard_map/ppermute | solution.py:270
  49.3 11.5 %collective-permute-start.7 = (bf16[384,2048]{1,0:T(8,128)(2,1)}, bf16[384,2048]{1,0:T(8,128)(2,1)}, u32[]{:S(2)}, u32[]{:S(2)}) collective-permute-start(bf16[384,2048]{1,0:T(8,128)(2,1)} %bitcast.32), channel_id=1, source_target_pairs={{0,1},{1,0},{2,3},{3,2},{4,5},{5,4},{6,7},{7,6},{8,9},{9,8},{10,11... | collective-permute-start | bytes 4718600 | tf_op jit(solution)/shard_map/ppermute | solution.py:270
  55.9 1.0 copy-start.4
  56.8 19.8 %all-to-all-start = ((bf16[16,8,6400]{2,1,0:T(8,128)(2,1)}), bf16[16,8,6400]{2,1,0:T(8,128)(2,1)S(1)}, u32[]{:S(2)}, u32[]{:S(2)}) async-start(bf16[16,8,6400]{2,1,0:T(8,128)(2,1)} %bitcast.4), calls=%async_computation | async-start | bytes 3276800 | tf_op jit(solution)/shard_map/all_to_all | solution.py:281
  76.7 5.7 %copy-start.3 = (bf16[16,8,6400]{2,1,0:T(8,128)(2,1)}, bf16[16,8,6400]{2,1,0:T(8,128)(2,1)S(1)}, u32[]{:S(2)}) copy-start(bf16[16,8,6400]{2,1,0:T(8,128)(2,1)S(1)} %all-to-all-done) | copy-start | bytes 4915204
  76.7 17.5 %all-to-all-start.3 = ((bf16[16,8,4096]{2,1,0:T(8,128)(2,1)}), bf16[16,8,4096]{2,1,0:T(8,128)(2,1)S(1)}, u32[]{:S(2)}, u32[]{:S(2)}) async-start(bf16[16,8,4096]{2,1,0:T(8,128)(2,1)} %bitcast.36), calls=%async_computation.3 | async-start | bytes 2097152 | tf_op jit(solution)/shard_map/all_to_all | solution.py:294
  94.2 4.8 %copy-start.2 = (s32[2]{0:T(128)S(1)}, s32[2]{0:T(128)}, u32[]{:S(2)}) copy-start(s32[2]{0:T(128)} %copy-done.1) | copy-start | bytes 28
  94.2 24.0 %all-to-all-start.1 = ((bf16[16,8,6400]{2,1,0:T(8,128)(2,1)}), bf16[16,8,6400]{2,1,0:T(8,128)(2,1)S(1)}, u32[]{:S(2)}, u32[]{:S(2)}) async-start(bf16[16,8,6400]{2,1,0:T(8,128)(2,1)} %bitcast.24), calls=%async_computation.1 | async-start | bytes 3276800 | tf_op jit(solution)/shard_map/all_to_all | solution.py:294
  99.9 13.0 %collective-permute-start.12 = (bf16[128,512]{1,0:T(8,128)(2,1)S(1)}, bf16[128,512]{1,0:T(8,128)(2,1)S(1)}, u32[]{:S(2)}, u32[]{:S(2)}) collective-permute-start(bf16[128,512]{1,0:T(8,128)(2,1)S(1)} %get-tuple-element.46), channel_id=1, source_target_pairs={{32,0},{225,1},{64,32},{1,33},{96,64},{33,65},{128,96},{65,97},{16... | collective-permute-start | bytes 393224 | tf_op jit(solution)/shard_map/ppermute | solution.py:315
  101.0 13.3 %collective-permute-start.16 = (bf16[128,512]{1,0:T(8,128)(2,1)S(1)}, bf16[128,512]{1,0:T(8,128)(2,1)S(1)}, u32[]{:S(2)}, u32[]{:S(2)}) collective-permute-start(bf16[128,512]{1,0:T(8,128)(2,1)S(1)} %get-tuple-element.50), channel_id=1, source_target_pairs={{32,0},{225,1},{64,32},{1,33},{96,64},{33,65},{128,96},{65,97},{16... | collective-permute-start | bytes 393224 | tf_op jit(solution)/shard_map/ppermute | solution.py:315
  108.3 9.3 %collective-permute-start.20 = (bf16[128,512]{1,0:T(8,128)(2,1)S(1)}, bf16[128,512]{1,0:T(8,128)(2,1)S(1)}, u32[]{:S(2)}, u32[]{:S(2)}) collective-permute-start(bf16[128,512]{1,0:T(8,128)(2,1)S(1)} %get-tuple-element.54), channel_id=1, source_target_pairs={{32,0},{225,1},{64,32},{1,33},{96,64},{33,65},{128,96},{65,97},{16... | collective-permute-start | bytes 393224 | tf_op jit(solution)/shard_map/ppermute | solution.py:315
  111.2 6.8 %collective-permute-start.24 = (bf16[128,512]{1,0:T(8,128)(2,1)S(1)}, bf16[128,512]{1,0:T(8,128)(2,1)S(1)}, u32[]{:S(2)}, u32[]{:S(2)}) collective-permute-start(bf16[128,512]{1,0:T(8,128)(2,1)S(1)} %get-tuple-element.58), channel_id=1, source_target_pairs={{32,0},{225,1},{64,32},{1,33},{96,64},{33,65},{128,96},{65,97},{16... | collective-permute-start | bytes 393224 | tf_op jit(solution)/shard_map/ppermute | solution.py:315
  112.9 8.6 %collective-permute-start.13 = (bf16[128,512]{1,0:T(8,128)(2,1)S(1)}, bf16[128,512]{1,0:T(8,128)(2,1)S(1)}, u32[]{:S(2)}, u32[]{:S(2)}) collective-permute-start(bf16[128,512]{1,0:T(8,128)(2,1)S(1)} %add_convert_fusion.12), channel_id=1, source_target_pairs={{32,0},{225,1},{64,32},{1,33},{96,64},{33,65},{128,96},{65,97},{16... | collective-permute-start | bytes 393224 | tf_op jit(solution)/shard_map/ppermute | solution.py:315
  114.3 5.6 %collective-permute-start.17 = (bf16[128,512]{1,0:T(8,128)(2,1)S(1)}, bf16[128,512]{1,0:T(8,128)(2,1)S(1)}, u32[]{:S(2)}, u32[]{:S(2)}) collective-permute-start(bf16[128,512]{1,0:T(8,128)(2,1)S(1)} %add_convert_fusion.9), channel_id=1, source_target_pairs={{32,0},{225,1},{64,32},{1,33},{96,64},{33,65},{128,96},{65,97},{16... | collective-permute-start | bytes 393224 | tf_op jit(solution)/shard_map/ppermute | solution.py:315
  117.6 8.6 %collective-permute-start.21 = (bf16[128,512]{1,0:T(8,128)(2,1)S(1)}, bf16[128,512]{1,0:T(8,128)(2,1)S(1)}, u32[]{:S(2)}, u32[]{:S(2)}) collective-permute-start(bf16[128,512]{1,0:T(8,128)(2,1)S(1)} %add_convert_fusion.6), channel_id=1, source_target_pairs={{32,0},{225,1},{64,32},{1,33},{96,64},{33,65},{128,96},{65,97},{16... | collective-permute-start | bytes 393224 | tf_op jit(solution)/shard_map/ppermute | solution.py:315
  118.1 13.4 %collective-permute-start.25 = (bf16[128,512]{1,0:T(8,128)(2,1)S(1)}, bf16[128,512]{1,0:T(8,128)(2,1)S(1)}, u32[]{:S(2)}, u32[]{:S(2)}) collective-permute-start(bf16[128,512]{1,0:T(8,128)(2,1)S(1)} %add_convert_fusion.3), channel_id=1, source_target_pairs={{32,0},{225,1},{64,32},{1,33},{96,64},{33,65},{128,96},{65,97},{16... | collective-permute-start | bytes 393224 | tf_op jit(solution)/shard_map/ppermute | solution.py:315
  119.9 12.7 %collective-permute-start.18 = (bf16[128,512]{1,0:T(8,128)(2,1)S(1)}, bf16[128,512]{1,0:T(8,128)(2,1)S(1)}, u32[]{:S(2)}, u32[]{:S(2)}) collective-permute-start(bf16[128,512]{1,0:T(8,128)(2,1)S(1)} %add_convert_fusion.8), channel_id=1, source_target_pairs={{32,0},{225,1},{64,32},{1,33},{96,64},{33,65},{128,96},{65,97},{16... | collective-permute-start | bytes 393224 | tf_op jit(solution)/shard_map/ppermute | solution.py:315
  121.6 11.2 %collective-permute-start.14 = (bf16[128,512]{1,0:T(8,128)(2,1)S(1)}, bf16[128,512]{1,0:T(8,128)(2,1)S(1)}, u32[]{:S(2)}, u32[]{:S(2)}) collective-permute-start(bf16[128,512]{1,0:T(8,128)(2,1)S(1)} %add_convert_fusion.11), channel_id=1, source_target_pairs={{32,0},{225,1},{64,32},{1,33},{96,64},{33,65},{128,96},{65,97},{16... | collective-permute-start | bytes 393224 | tf_op jit(solution)/shard_map/ppermute | solution.py:315
  126.3 13.0 %collective-permute-start.22 = (bf16[128,512]{1,0:T(8,128)(2,1)S(1)}, bf16[128,512]{1,0:T(8,128)(2,1)S(1)}, u32[]{:S(2)}, u32[]{:S(2)}) collective-permute-start(bf16[128,512]{1,0:T(8,128)(2,1)S(1)} %add_convert_fusion.5), channel_id=1, source_target_pairs={{32,0},{225,1},{64,32},{1,33},{96,64},{33,65},{128,96},{65,97},{16... | collective-permute-start | bytes 393224 | tf_op jit(solution)/shard_map/ppermute | solution.py:315
  131.5 7.9 %collective-permute-start.26 = (bf16[128,512]{1,0:T(8,128)(2,1)S(1)}, bf16[128,512]{1,0:T(8,128)(2,1)S(1)}, u32[]{:S(2)}, u32[]{:S(2)}) collective-permute-start(bf16[128,512]{1,0:T(8,128)(2,1)S(1)} %add_convert_fusion.2), channel_id=1, source_target_pairs={{32,0},{225,1},{64,32},{1,33},{96,64},{33,65},{128,96},{65,97},{16... | collective-permute-start | bytes 393224 | tf_op jit(solution)/shard_map/ppermute | solution.py:315
  132.7 6.9 %collective-permute-start.19 = (bf16[128,512]{1,0:T(8,128)(2,1)S(1)}, bf16[128,512]{1,0:T(8,128)(2,1)S(1)}, u32[]{:S(2)}, u32[]{:S(2)}) collective-permute-start(bf16[128,512]{1,0:T(8,128)(2,1)S(1)} %add_convert_fusion.7), channel_id=1, source_target_pairs={{32,0},{225,1},{64,32},{1,33},{96,64},{33,65},{128,96},{65,97},{16... | collective-permute-start | bytes 393224 | tf_op jit(solution)/shard_map/ppermute | solution.py:315
  132.8 8.4 %collective-permute-start.15 = (bf16[128,512]{1,0:T(8,128)(2,1)S(1)}, bf16[128,512]{1,0:T(8,128)(2,1)S(1)}, u32[]{:S(2)}, u32[]{:S(2)}) collective-permute-start(bf16[128,512]{1,0:T(8,128)(2,1)S(1)} %add_convert_fusion.10), channel_id=1, source_target_pairs={{32,0},{225,1},{64,32},{1,33},{96,64},{33,65},{128,96},{65,97},{16... | collective-permute-start | bytes 393224 | tf_op jit(solution)/shard_map/ppermute | solution.py:315
  139.3 5.1 %collective-permute-start.23 = (bf16[128,512]{1,0:T(8,128)(2,1)S(1)}, bf16[128,512]{1,0:T(8,128)(2,1)S(1)}, u32[]{:S(2)}, u32[]{:S(2)}) collective-permute-start(bf16[128,512]{1,0:T(8,128)(2,1)S(1)} %add_convert_fusion.4), channel_id=1, source_target_pairs={{32,0},{225,1},{64,32},{1,33},{96,64},{33,65},{128,96},{65,97},{16... | collective-permute-start | bytes 393224 | tf_op jit(solution)/shard_map/ppermute | solution.py:315
  139.4 6.4 %collective-permute-start.27 = (bf16[128,512]{1,0:T(8,128)(2,1)S(1)}, bf16[128,512]{1,0:T(8,128)(2,1)S(1)}, u32[]{:S(2)}, u32[]{:S(2)}) collective-permute-start(bf16[128,512]{1,0:T(8,128)(2,1)S(1)} %add_convert_fusion.1), channel_id=1, source_target_pairs={{32,0},{225,1},{64,32},{1,33},{96,64},{33,65},{128,96},{65,97},{16... | collective-permute-start | bytes 393224 | tf_op jit(solution)/shard_map/ppermute | solution.py:315
  146.7 7.9 %collective-permute-start.28 = (bf16[128,1024]{1,0:T(8,128)(2,1)S(1)}, bf16[128,1024]{1,0:T(8,128)(2,1)S(1)}, u32[]{:S(2)}, u32[]{:S(2)}) collective-permute-start(bf16[128,1024]{1,0:T(8,128)(2,1)S(1)} %get-tuple-element.60), channel_id=1, source_target_pairs={{0,1},{1,0},{2,3},{3,2},{4,5},{5,4},{6,7},{7,6},{8,9},{9,8},{10,11... | collective-permute-start | bytes 786440 | tf_op jit(solution)/shard_map/ppermute | solution.py:317
where the time goes:
time: 156 us; the launch traced here: 155 us
  starting transfers between devices  91.4 us (59%)
  waiting for transfers between devices  32.6 us (21%)
  Pallas kernels  29 us (19%)
    ppermute x16, starting transfers between devices, staged(): received = [lax.ppermute(v, ('z', 'half'), back) for v in outs]  32.5 us
    ppermute x8, starting transfers between devices, staged(): held[d] = [lax.ppermute(v, ('z', 'half'), forth) for v in held[d - 1]]  22.3 us
    pallas_call x2, Pallas kernels, staged(): kernel(functools.partial(expert_body, chunk), [((size, lanes), BF16)], [S...  17.6 us
    all_to_all x2, waiting for transfers between devices, staged(): lax.all_to_all(sent.reshape(PLANE, SUB, lanes), ('x', 'y'), 0, 0, tiled=T...  12 us
    all_to_all x2, starting transfers between devices, staged(): lax.all_to_all(sent.reshape(PLANE, SUB, lanes), ('x', 'y'), 0, 0, tiled=T...  10.6 us
    all_to_all x2, starting transfers between devices, staged(): lax.all_to_all(result.reshape(PLANE, SUB, lanes), ('x', 'y'), 0, 0, tiled...  10.4 us
    ppermute x16, waiting for transfers between devices, staged(): received = [lax.ppermute(v, ('z', 'half'), back) for v in outs]  9.67 us
    ppermute x8, waiting for transfers between devices, staged(): held[d] = [lax.ppermute(v, ('z', 'half'), forth) for v in held[d - 1]]  7.86 us
  transfers between devices with their start and end apart: 33, of which 15 were waited for; matrix products, arithmetic and copies ran while one was open for 0% of the time, Pallas kernels for 17%

commit v1 on v0

v1 whole, which is shorter than its diff:
```python
import functools

import jax
import jax.numpy as jnp
from jax import lax
from jax.experimental import pallas as pl
from jax.experimental.pallas import tpu as pltpu
from jax.sharding import Mesh, PartitionSpec as P


F32 = jnp.float32
BF16 = jnp.bfloat16
CAP = 10
TOK = 128
WIDE = 2048
HALF = 1024
PART = 512
FH = 384
PLANE = 16
SUB = 8
LEFT = WIDE // SUB
PIECES = {0: 5, 1: 10, 2: 10, 3: 10, 4: 5}
CHUNKS = ((0,), (1, 2), (3, 4))
TAKES = ((0, 1), (2,))
EXPERT_VMEM = 56
ROUTE_VMEM = 58


def iota(shape, dim):
    return lax.broadcasted_iota(jnp.int32, shape, dim)


def parts_of(d):
    return PIECES[d] // SUB * SUB, PIECES[d] % SUB


def lanes_of(d):
    tile, rest = parts_of(d)
    return tile // SUB * WIDE + rest * LEFT


def width_of(chunk):
    return sum(lanes_of(d) for d in chunk)


def route_body(tok_ref, ids_ref, w_ref, out_ref):
    ids = ids_ref[...]
    experts = iota((128, TOK), 0)
    named = jnp.zeros((128, TOK), F32)
    for k in range(8):
        named = jnp.where(ids[k : k + 1, :] == experts, 1.0, named)
    before = jnp.where(iota((TOK, TOK), 0) < iota((TOK, TOK), 1), 1.0, 0.0)
    count = jnp.dot(named.astype(BF16), before.astype(BF16), preferred_element_type=F32)
    ranks = [
        jnp.sum(jnp.where(ids[k : k + 1, :] == experts, count, 0.0), axis=0, keepdims=True)
        for k in range(8)
    ]
    w = w_ref[...]
    hi = w.astype(BF16)
    out_ref[0:TOK, :] = tok_ref[...]
    out_ref[TOK : TOK + 8, 0:128] = ids.astype(F32).astype(BF16)
    out_ref[TOK : TOK + 8, 128:256] = jnp.concatenate(ranks, axis=0).astype(BF16)
    out_ref[TOK : TOK + 8, 256:384] = hi
    out_ref[TOK : TOK + 8, 384:512] = (w - hi.astype(F32)).astype(BF16)
    out_ref[TOK : TOK + 8, 512:1024] = jnp.zeros((8, 512), BF16)


def slot_table(info, first, half, slots, values):
    ids = info[:, 0:128].astype(F32)
    rank = info[:, 128:256].astype(F32)
    mine = iota((PLANE, TOK), 0).astype(F32) + first.astype(F32)
    slot = jnp.full((PLANE, TOK), -1000.0, F32)
    picked = [jnp.zeros((PLANE, TOK), F32) for _ in values]
    for k in range(8):
        hit = ids[k : k + 1, :] == mine
        slot = jnp.where(hit, rank[k : k + 1, :], slot)
        for i, at in enumerate(values):
            value = info[:, at : at + 128].astype(F32)
            picked[i] = jnp.where(hit, value[k : k + 1, :], picked[i])
    slot = slot.astype(jnp.int32)
    if slots < CAP:
        slot = slot - half * slots
        slot = jnp.where((slot >= 0) & (slot < slots), slot, -1000)
    return slot, picked


def placed(slot, d, value=None):
    tile, rest = parts_of(d)
    one = 1.0 if value is None else value
    out = []
    if tile:
        hit = slot[:, None, :] == iota((PLANE, SUB, TOK), 1)
        three = one if value is None else value[:, None, :]
        out.append(jnp.where(hit, three, 0.0).astype(BF16).reshape(PLANE * SUB, TOK))
    for s in range(tile, tile + rest):
        out.append(jnp.where(slot == s, one, 0.0).astype(BF16))
    return jnp.concatenate(out, axis=0)


def swapped():
    row, column = iota((PLANE * SUB, PLANE * SUB), 0), iota((PLANE * SUB, PLANE * SUB), 1)
    return jnp.where(column == (row & (PLANE - 1)) * SUB + (row >> 4), 1.0, 0.0).astype(BF16)


def unswapped():
    row, column = iota((PLANE * SUB, PLANE * SUB), 0), iota((PLANE * SUB, PLANE * SUB), 1)
    return jnp.where(row == (column & (PLANE - 1)) * SUB + (column >> 4), 1.0, 0.0).astype(BF16)


def packed(rows, number):
    z = jnp.concatenate(
        [
            jnp.concatenate(
                [rows[s * PLANE : (s + 1) * PLANE, q * LEFT : (q + 1) * LEFT] for s in range(number)],
                axis=1,
            )
            for q in range(SUB)
        ],
        axis=0,
    )
    return jnp.dot(unswapped(), z, preferred_element_type=F32).astype(BF16)


def unpacked(rows, number):
    z = jnp.dot(swapped(), rows, preferred_element_type=F32).astype(BF16)
    return [
        jnp.concatenate(
            [z[q * PLANE : (q + 1) * PLANE, s * LEFT : (s + 1) * LEFT] for q in range(SUB)], axis=1
        )
        for s in range(number)
    ]


def dispatch_body(chunk, scal_ref, *refs):
    number = len(chunk)
    out_ref = refs[2 * number]
    at = 0
    for i, d in enumerate(chunk):
        a_ref, b_ref = refs[2 * i], refs[2 * i + 1]
        tile, rest = parts_of(d)
        info = a_ref[TOK : TOK + 8, 0:512]
        refs[2 * number + 1 + i][...] = info
        slot, _ = slot_table(info, scal_ref[0], scal_ref[1], PIECES[d], ())
        onehot = placed(slot, d)
        rows = jnp.concatenate(
            [
                jnp.dot(onehot, ref[0:TOK, :], preferred_element_type=F32).astype(BF16)
                for ref in (a_ref, b_ref)
            ],
            axis=1,
        )
        if tile:
            out_ref[:, at : at + WIDE] = rows[0 : PLANE * tile, :]
            at += WIDE
        out_ref[:, at : at + rest * LEFT] = packed(rows[PLANE * tile :, :], rest)
        at += rest * LEFT


def places(chunks):
    out = []
    for n, chunk in enumerate(chunks):
        at = 0
        for d in chunk:
            out.append((n, d, at))
            at += lanes_of(d)
    return out


def expert_body(chunks, scal_ref, *refs):
    number = len(chunks)
    xs = refs[:number]
    gm_ref, gp_ref, um_ref, up_ref, dm_ref, dp_ref = refs[number : number + 6]
    outs = refs[number + 6 : 2 * number + 6]
    wm, wp, wd, sems = refs[2 * number + 6 :]
    half = scal_ref[1]
    copies = []
    for side in range(2):
        at = pl.multiple_of((half if side == 0 else 1 - half) * HALF, HALF)
        here = pl.ds(at, HALF)
        to = pl.ds(side * HALF, HALF)
        for i, (src, dst, lane) in enumerate(((gm_ref, wm, 0), (um_ref, wm, FH), (gp_ref, wp, 0), (up_ref, wp, FH))):
            copies.append((i // 2 * 2 + side, src.at[here, :], dst.at[to, pl.ds(lane, FH)]))
        for src, row in ((dm_ref, 0), (dp_ref, FH)):
            copies.append((4, src.at[:, here], wd.at[pl.ds(row, FH), to]))
    copies.sort(key=lambda c: c[0])
    copies = [pltpu.make_async_copy(src, dst, sems.at[n]) for n, (_, src, dst) in enumerate(copies)]
    for c in copies:
        c.start()
    spots = places(chunks)
    blocks = [xs[n][:, at : at + WIDE] for n, d, at in spots if parts_of(d)[0]]
    for n, d, at in spots:
        tile, rest = parts_of(d)
        at += tile // SUB * WIDE
        blocks += unpacked(xs[n][:, at : at + rest * LEFT], rest)
    x = jnp.concatenate(blocks, axis=0)
    hidden = []
    for i, w in enumerate((wm, wp)):
        both = None
        for side in range(2):
            for c in copies[4 * i + 2 * side : 4 * i + 2 * side + 2]:
                c.wait()
            to = slice(side * HALF, (side + 1) * HALF)
            part = jnp.dot(x[:, to], w[to, :], preferred_element_type=F32)
            both = part if both is None else both + part
        gate = both[:, :FH]
        hidden.append((gate / (1.0 + jnp.exp(-gate)) * both[:, FH:]).astype(BF16))
    for c in copies[8:]:
        c.wait()
    y = jnp.dot(jnp.concatenate(hidden, axis=1), wd[...], preferred_element_type=F32).astype(BF16)
    size = PLANE * SUB
    row = 0
    for n, d, at in spots:
        if parts_of(d)[0]:
            outs[n][:, at : at + WIDE] = y[row : row + size, :]
            row += size
    for n, d, at in spots:
        tile, rest = parts_of(d)
        at += tile // SUB * WIDE
        outs[n][:, at : at + rest * LEFT] = packed(y[row : row + rest * PLANE, :], rest)
        row += rest * PLANE


def combine_body(d, last, scal_ref, info_ref, y_ref, *refs):
    tile, rest = parts_of(d)
    slot, values = slot_table(info_ref[...], scal_ref[0], scal_ref[1], PIECES[d], (256, 384))
    weights = jnp.concatenate([placed(slot, d, value) for value in values], axis=0)
    rows = [y_ref[:, 0:WIDE]] if tile else []
    rows += unpacked(y_ref[:, tile // SUB * WIDE :], rest)
    rows = jnp.concatenate(rows * 2, axis=0)
    total = lax.dot_general(weights, rows, (((0,), (0,)), ((), ())), preferred_element_type=F32)
    parts = [total[:, p * PART : (p + 1) * PART] for p in range(4)]
    if last:
        parts = [part + refs[p][...].astype(F32) for p, part in enumerate(parts)]
        for side in range(2):
            out = refs[4 + side]
            out[...] = jnp.concatenate(parts[2 * side : 2 * side + 2], axis=1).astype(out.dtype)
    else:
        for p in range(4):
            refs[p][...] = parts[p].astype(refs[p].dtype)


def whole(shape):
    return pl.BlockSpec(shape, lambda i: (0,) * len(shape))


def lane_block(shape, at):
    return pl.BlockSpec(shape, lambda i: (0, at))


SMEM = pl.BlockSpec(memory_space=pltpu.SMEM)
HBM = pl.BlockSpec(memory_space=pltpu.HBM)


def kernel(body, out, in_specs, scratch=(), vmem=16):
    return pl.pallas_call(
        body,
        out_shape=[jax.ShapeDtypeStruct(*o) for o in out],
        grid=(1,),
        in_specs=in_specs,
        out_specs=[whole(o[0]) for o in out],
        scratch_shapes=list(scratch),
        compiler_params=pltpu.CompilerParams(vmem_limit_bytes=vmem * 1024 * 1024),
    )


def staged(tokens, gate_weights, expert_ids, w_gate, w_up, w_down):
    z = lax.axis_index("z")
    half = lax.axis_index("half")
    zs = lax.axis_size("z")
    scal = jnp.stack([z * PLANE, half]).astype(jnp.int32)
    swap = [(0, 1), (1, 0)]
    forth = []
    for i in range(zs):
        forth.append((i * 2, (i + 1) % zs * 2))
        forth.append((i * 2 + 1, (i - 1) % zs * 2 + 1))
    back = [(b, a) for a, b in forth]
    size = PLANE * SUB

    side = (TOK, HALF)
    other = lax.ppermute(tokens, "half", swap)
    (own,) = kernel(
        route_body,
        [((TOK + 8, HALF), BF16)],
        [whole(side), whole((8, TOK)), whole((8, TOK))],
        vmem=ROUTE_VMEM,
    )(tokens, expert_ids.T, gate_weights.T)
    held = {0: [own, other]}
    for d in range(1, 5):
        held[d] = [lax.ppermute(v, ("z", "half"), forth) for v in held[d - 1]]
    mine = (w_gate[0], w_up[0], w_down[0])
    gated = lax.optimization_barrier((other,) + mine)
    theirs = [lax.ppermute(w, "half", swap) for w in gated[1:]]

    infos = {}
    gots = []
    for chunk in CHUNKS:
        width = width_of(chunk)
        arrays = [v for d in chunk for v in held[d]]
        sent, *seen = kernel(
            functools.partial(dispatch_body, chunk),
            [((size, width), BF16)] + [((8, 512), BF16) for _ in chunk],
            [SMEM] + [whole(v.shape) for v in arrays],
        )(scal, *arrays)
        infos.update(zip(chunk, seen))
        got = lax.all_to_all(sent.reshape(PLANE, SUB, width), ("x", "y"), 0, 0, tiled=True)
        gots.append(got.reshape(size, width))
    results = {}
    for takes in TAKES:
        arrays = [gots[n] for n in takes]
        made = kernel(
            functools.partial(expert_body, [CHUNKS[n] for n in takes]),
            [(v.shape, BF16) for v in arrays],
            [SMEM] + [whole(v.shape) for v in arrays] + [HBM] * 6,
            (
                pltpu.VMEM((WIDE, 2 * FH), BF16),
                pltpu.VMEM((WIDE, 2 * FH), BF16),
                pltpu.VMEM((2 * FH, WIDE), BF16),
                pltpu.SemaphoreType.DMA((12,)),
            ),
            EXPERT_VMEM,
        )(scal, *arrays, mine[0], theirs[0], mine[1], theirs[1], mine[2], theirs[2])
        results.update(zip(takes, made))

    received = []
    for n in (2, 1, 0):
        chunk = CHUNKS[n]
        width = width_of(chunk)
        value = lax.all_to_all(results[n].reshape(PLANE, SUB, width), ("x", "y"), 0, 0, tiled=True)
        value = value.reshape(size, width)
        for d in reversed(chunk):
            lanes = lanes_of(d)
            at = sum(lanes_of(e) for e in chunk if e < d)
            last = d == 0
            extra = received if last else []
            outs = kernel(
                functools.partial(combine_body, d, last),
                [(side, F32), (side, BF16)] if last else [((TOK, PART), F32 if received else BF16)] * 4,
                [SMEM, whole((8, 512)), lane_block((size, lanes), at // lanes)]
                + [whole((TOK, PART)) for _ in extra],
            )(scal, infos[d], value, *extra)
            if not last:
                if received:
                    outs = [(v + r.astype(F32)).astype(BF16) for v, r in zip(outs, received)]
                received = [lax.ppermute(v, ("z", "half"), back) for v in outs]
    kept, given = outs
    return (kept + lax.ppermute(given, "half", swap).astype(F32)).astype(BF16)


def solution(mesh):
    spaced = Mesh(mesh.devices.reshape(8, 4, 4, 2), ("z", "x", "y", "half"))
    ep = ("z", "x", "y")
    specs = (
        P(ep, "half"),
        P(ep, None),
        P(ep, None),
        P(ep, None, "half"),
        P(ep, None, "half"),
        P(ep, "half", None),
    )
    return jax.shard_map(
        staged, mesh=spaced, in_specs=specs, out_specs=P(ep, "half"), check_vma=False
    )
```

time: 156 us -> 168 us (1.077)
  the two profiles are of different devices: /device:TPU:1 before, /device:TPU:24 now
where the time goes in v1:
time: 168 us; the launch traced here: 166 us
  waiting for transfers between devices  67.4 us (40%)
  starting transfers between devices  62 us (37%)
  Pallas kernels  32.4 us (19%)
  other arithmetic  2.15 us (1%)
    ppermute x8, waiting for transfers between devices, staged(): held[d] = [lax.ppermute(v, ('z', 'half'), forth) for v in held[d - 1]]  24.4 us
    all_to_all x3, starting transfers between devices, staged(): lax.all_to_all(sent.reshape(PLANE, SUB, width), ('x', 'y'), 0, 0, tiled=T...  20.9 us
    all_to_all x3, starting transfers between devices, staged(): lax.all_to_all(results[n].reshape(PLANE, SUB, width), ('x', 'y'), 0, 0, t...  18.2 us
    pallas_call x2, Pallas kernels, staged(): kernel(functools.partial(expert_body, [CHUNKS[n] for n in takes]), [(v.sh...  17.9 us
    all_to_all x3, waiting for transfers between devices, staged(): lax.all_to_all(sent.reshape(PLANE, SUB, width), ('x', 'y'), 0, 0, tiled=T...  17.9 us
    all_to_all x3, waiting for transfers between devices, staged(): lax.all_to_all(results[n].reshape(PLANE, SUB, width), ('x', 'y'), 0, 0, t...  14.8 us
    ppermute x16, starting transfers between devices, staged(): received = [lax.ppermute(v, ('z', 'half'), back) for v in outs]  14.8 us
    ppermute x16, waiting for transfers between devices, staged(): received = [lax.ppermute(v, ('z', 'half'), back) for v in outs]  8.76 us
  transfers between devices with their start and end apart: 35, of which 15 were waited for; matrix products, arithmetic and copies ran while one was open for 1% of the time, Pallas kernels for 19%

profile of v1, /device:TPU:24, one launch (start us, length us, event | category | flops | bytes accessed | tf_op | source)
XLA Modules:
  0.0 165.8 jit_solution(12265499985780342892)
XLA Ops:
  0.0 1.9 %shard_map.64.refs_0_ = bf16[136,1024]{1,0:T(8,128)(2,1)} custom-call(bf16[128,1024]{1,0:T(8,128)(2,1)} %tok_ref.1, s32[8,128]{1,0:T(8,128)} %bitcast.36, f32[8,128]{1,0:T(8,128)} %bitcast.37), custom_call_target="tpu_custom_call" | custom-call | tf_op jit(solution)/shard_map/pallas_call | solution.py:281
  1.9 1.9 %collective-permute-start.1 = (bf16[136,1024]{1,0:T(8,128)(2,1)}, bf16[136,1024]{1,0:T(8,128)(2,1)S(1)}, u32[]{:S(2)}, u32[]{:S(2)}) collective-permute-start(bf16[136,1024]{1,0:T(8,128)(2,1)} %shard_map.64.refs_0_), channel_id=1, source_target_pairs={{0,32},{1,225},{32,64},{33,1},{64,96},{65,33},{96,128},{97,65},{12... | collective-permute-start | bytes 835592 | tf_op jit(solution)/shard_map/ppermute | solution.py:289
  3.8 1.9 %collective-permute-start.2 = (bf16[128,1024]{1,0:T(8,128)(2,1)S(1)}, bf16[128,1024]{1,0:T(8,128)(2,1)S(1)}, u32[]{:S(2)}, u32[]{:S(2)}) collective-permute-start(bf16[128,1024]{1,0:T(8,128)(2,1)S(1)} %collective-permute-done.refs_1_), channel_id=1, source_target_pairs={{0,32},{1,225},{32,64},{33,1},{64,96},{65,33},{96,128},{97,65},{12... | collective-permute-start | bytes 786440 | tf_op jit(solution)/shard_map/ppermute | solution.py:289
  5.7 6.8 %collective-permute-done.1.refs_0_ = bf16[136,1024]{1,0:T(8,128)(2,1)S(1)} collective-permute-done((bf16[136,1024]{1,0:T(8,128)(2,1)}, bf16[136,1024]{1,0:T(8,128)(2,1)S(1)}, u32[]{:S(2)}, u32[]{:S(2)}) %collective-permute-start.1) | collective-permute-done | bytes 278560 | tf_op jit(solution)/shard_map/ppermute | solution.py:289
  12.5 2.8 %collective-permute-done.2.refs_1_ = bf16[128,1024]{1,0:T(8,128)(2,1)S(1)} collective-permute-done((bf16[128,1024]{1,0:T(8,128)(2,1)S(1)}, bf16[128,1024]{1,0:T(8,128)(2,1)S(1)}, u32[]{:S(2)}, u32[]{:S(2)}) %collective-permute-start.2) | collective-permute-done | bytes 262176 | tf_op jit(solution)/shard_map/ppermute | solution.py:289
  15.3 4.9 %collective-permute-done.3.refs_2_ = bf16[136,1024]{1,0:T(8,128)(2,1)S(1)} collective-permute-done((bf16[136,1024]{1,0:T(8,128)(2,1)S(1)}, bf16[136,1024]{1,0:T(8,128)(2,1)S(1)}, u32[]{:S(2)}, u32[]{:S(2)}) %collective-permute-start.3) | collective-permute-done | bytes 278560 | tf_op jit(solution)/shard_map/ppermute | solution.py:289
  20.3 2.8 %collective-permute-done.4.refs_3_ = bf16[128,1024]{1,0:T(8,128)(2,1)S(1)} collective-permute-done((bf16[128,1024]{1,0:T(8,128)(2,1)S(1)}, bf16[128,1024]{1,0:T(8,128)(2,1)S(1)}, u32[]{:S(2)}, u32[]{:S(2)}) %collective-permute-start.4) | collective-permute-done | bytes 262176 | tf_op jit(solution)/shard_map/ppermute | solution.py:289
  23.1 1.0 copy-done
  24.1 1.7 %shard_map.65 = (bf16[128,1280]{1,0:T(8,128)(2,1)}, bf16[8,512]{1,0:T(8,128)(2,1)S(1)}) custom-call(s32[2]{0:T(128)S(1)} %pad_add_fusion.scal_ref, bf16[136,1024]{1,0:T(8,128)(2,1)S(1)} %copy-done, bf16[128,1024]{1,0:T(8,128)(2,1)S(1)} %collective-permute-done.refs_1_), custom_call_target="tpu_custom_call" | custom-call | tf_op jit(solution)/shard_map/pallas_call | solution.py:299
  25.8 7.2 %all-to-all-start = ((bf16[16,8,1280]{2,1,0:T(8,128)(2,1)}), bf16[16,8,1280]{2,1,0:T(8,128)(2,1)}, u32[]{:S(2)}, u32[]{:S(2)}) async-start(bf16[16,8,1280]{2,1,0:T(8,128)(2,1)} %bitcast.4), calls=%async_computation | async-start | bytes 655360 | tf_op jit(solution)/shard_map/all_to_all | solution.py:305
  33.1 3.4 %collective-permute-start.11 = (bf16[128,1024]{1,0:T(8,128)(2,1)S(1)}, bf16[128,1024]{1,0:T(8,128)(2,1)S(1)}, u32[]{:S(2)}, u32[]{:S(2)}) collective-permute-start(bf16[128,1024]{1,0:T(8,128)(2,1)S(1)} %collective-permute-done.9.refs_1_), channel_id=1, source_target_pairs={{0,32},{1,225},{32,64},{33,1},{64,96},{65,33},{96,128},{97,65},{12... | collective-permute-start | bytes 786440 | tf_op jit(solution)/shard_map/ppermute | solution.py:289
  36.5 4.3 %collective-permute-done.10.refs_2_ = bf16[136,1024]{1,0:T(8,128)(2,1)S(1)} collective-permute-done((bf16[136,1024]{1,0:T(8,128)(2,1)S(1)}, bf16[136,1024]{1,0:T(8,128)(2,1)S(1)}, u32[]{:S(2)}, u32[]{:S(2)}) %collective-permute-start.10) | collective-permute-done | bytes 278560 | tf_op jit(solution)/shard_map/ppermute | solution.py:289
  40.8 2.8 %collective-permute-done.11.refs_3_ = bf16[128,1024]{1,0:T(8,128)(2,1)S(1)} collective-permute-done((bf16[128,1024]{1,0:T(8,128)(2,1)S(1)}, bf16[128,1024]{1,0:T(8,128)(2,1)S(1)}, u32[]{:S(2)}, u32[]{:S(2)}) %collective-permute-start.11) | collective-permute-done | bytes 262176 | tf_op jit(solution)/shard_map/ppermute | solution.py:289
  43.6 2.3 %shard_map.70 = (bf16[128,3840]{1,0:T(8,128)(2,1)}, bf16[8,512]{1,0:T(8,128)(2,1)S(1)}, bf16[8,512]{1,0:T(8,128)(2,1)S(1)}) custom-call(s32[2]{0:T(128)S(1)} %pad_add_fusion.scal_ref, bf16[136,1024]{1,0:T(8,128)(2,1)S(1)} %collective-permute-done.8.refs_0_, bf16[128,1024]{1,0:T(8,128)(2,1)S(1)} %collective-permute-done.9.refs_1_, ...), custom_call_target="tpu_custom_call" | custom-call | tf_op jit(solution)/shard_map/pallas_call | solution.py:299
  46.0 7.2 %all-to-all-start.4 = ((bf16[16,8,3840]{2,1,0:T(8,128)(2,1)}), bf16[16,8,3840]{2,1,0:T(8,128)(2,1)}, u32[]{:S(2)}, u32[]{:S(2)}) async-start(bf16[16,8,3840]{2,1,0:T(8,128)(2,1)} %bitcast.15), calls=%async_computation.4 | async-start | bytes 1966080 | tf_op jit(solution)/shard_map/all_to_all | solution.py:305
  53.9 2.5 %shard_map.66 = (bf16[128,5120]{1,0:T(8,128)(2,1)}, bf16[8,512]{1,0:T(8,128)(2,1)S(1)}, bf16[8,512]{1,0:T(8,128)(2,1)S(1)}) custom-call(s32[2]{0:T(128)S(1)} %pad_add_fusion.scal_ref, bf16[136,1024]{1,0:T(8,128)(2,1)S(1)} %collective-permute-done.1.refs_0_, bf16[128,1024]{1,0:T(8,128)(2,1)S(1)} %collective-permute-done.2.refs_1_, ...), custom_call_target="tpu_custom_call" | custom-call | tf_op jit(solution)/shard_map/pallas_call | solution.py:299
  56.4 9.8 %all-to-all-done.4 = bf16[16,8,3840]{2,1,0:T(8,128)(2,1)} async-done(((bf16[16,8,3840]{2,1,0:T(8,128)(2,1)}), bf16[16,8,3840]{2,1,0:T(8,128)(2,1)}, u32[]{:S(2)}, u32[]{:S(2)}) %all-to-all-start.4) | async-done | bytes 983072 | tf_op jit(solution)/shard_map/all_to_all | solution.py:305
  66.2 6.5 %all-to-all-start.1 = ((bf16[16,8,5120]{2,1,0:T(8,128)(2,1)}), bf16[16,8,5120]{2,1,0:T(8,128)(2,1)}, u32[]{:S(2)}, u32[]{:S(2)}) async-start(bf16[16,8,5120]{2,1,0:T(8,128)(2,1)} %bitcast.6), calls=%async_computation.1 | async-start | bytes 2621440 | tf_op jit(solution)/shard_map/all_to_all | solution.py:305
  72.7 7.8 %shard_map.71 = bf16[128,3840]{1,0:T(8,128)(2,1)} custom-call(s32[2]{0:T(128)} %copy-done.3, bf16[128,3840]{1,0:T(8,128)(2,1)} %bitcast.16.refs_0_, bf16[2048,384]{1,0:T(8,128)(2,1)} %bitcast.24, bf16[2048,384]{1,0:T(8,128)(2,1)} %collective-permute-done.5.refs_3_.refs_2_, bf16[2048,384]{1,0:T(8,128)(2,1)} %bitcast.28, ...), custom_call_target="tpu_custom_call" | custom-call | tf_op jit(solution)/shard_map/pallas_call | solution.py:310
  80.5 8.0 %all-to-all-done.1 = bf16[16,8,5120]{2,1,0:T(8,128)(2,1)} async-done(((bf16[16,8,5120]{2,1,0:T(8,128)(2,1)}), bf16[16,8,5120]{2,1,0:T(8,128)(2,1)}, u32[]{:S(2)}, u32[]{:S(2)}) %all-to-all-start.1) | async-done | bytes 1310752 | tf_op jit(solution)/shard_map/all_to_all | solution.py:305
  88.6 6.0 %all-to-all-start.5 = ((bf16[16,8,3840]{2,1,0:T(8,128)(2,1)}), bf16[16,8,3840]{2,1,0:T(8,128)(2,1)S(1)}, u32[]{:S(2)}, u32[]{:S(2)}) async-start(bf16[16,8,3840]{2,1,0:T(8,128)(2,1)} %bitcast.33), calls=%async_computation.5 | async-start | bytes 1966080 | tf_op jit(solution)/shard_map/all_to_all | solution.py:328
  94.5 10.1 %shard_map.67 = (bf16[128,1280]{1,0:T(8,128)(2,1)}, bf16[128,5120]{1,0:T(8,128)(2,1)}) custom-call(s32[2]{0:T(128)} %copy-done.3, bf16[128,1280]{1,0:T(8,128)(2,1)} %bitcast.5.refs_0_, bf16[128,5120]{1,0:T(8,128)(2,1)} %bitcast.7.refs_1_, bf16[2048,384]{1,0:T(8,128)(2,1)} %bitcast.25, bf16[2048,384]{1,0:T(8,128)(2,1)} %collective-permute-done.5.refs_3_.refs_2_, ...), custom_call_target="tpu_custom_call" | custom-call | tf_op jit(solution)/shard_map/pallas_call | solution.py:310
  104.7 2.8 %all-to-all-done.5 = bf16[16,8,3840]{2,1,0:T(8,128)(2,1)S(1)} async-done(((bf16[16,8,3840]{2,1,0:T(8,128)(2,1)}), bf16[16,8,3840]{2,1,0:T(8,128)(2,1)S(1)}, u32[]{:S(2)}, u32[]{:S(2)}) %all-to-all-start.5) | async-done | bytes 983072 | tf_op jit(solution)/shard_map/all_to_all | solution.py:328
  107.4 6.0 %all-to-all-start.3 = ((bf16[16,8,5120]{2,1,0:T(8,128)(2,1)}), bf16[16,8,5120]{2,1,0:T(8,128)(2,1)S(1)}, u32[]{:S(2)}, u32[]{:S(2)}) async-start(bf16[16,8,5120]{2,1,0:T(8,128)(2,1)} %bitcast.34), calls=%async_computation.3 | async-start | bytes 2621440 | tf_op jit(solution)/shard_map/all_to_all | solution.py:328
  113.5 1.7 %shard_map.73 = (bf16[128,512]{1,0:T(8,128)(2,1)}, bf16[128,512]{1,0:T(8,128)(2,1)}, bf16[128,512]{1,0:T(8,128)(2,1)}, bf16[128,512]{1,0:T(8,128)(2,1)}) custom-call(s32[2]{0:T(128)S(1)} %copy-done.4, bf16[8,512]{1,0:T(8,128)(2,1)S(1)} %get-tuple-element.51.info_ref, bf16[128,3840]{1,0:T(8,128)(2,1)S(1)} %bitcast.21), custom_call_target="tpu_custom_call" | custom-call | tf_op jit(solution)/shard_map/pallas_call | solution.py:335
  115.2 1.0 collective-permute-start.12
  116.2 1.1 shard_map.72
  117.3 0.7 copy-done.1
  118.1 12.0 %all-to-all-done.3 = bf16[16,8,5120]{2,1,0:T(8,128)(2,1)S(1)} async-done(((bf16[16,8,5120]{2,1,0:T(8,128)(2,1)}), bf16[16,8,5120]{2,1,0:T(8,128)(2,1)S(1)}, u32[]{:S(2)}, u32[]{:S(2)}) %all-to-all-start.3) | async-done | bytes 1310752 | tf_op jit(solution)/shard_map/all_to_all | solution.py:328
  130.1 6.2 %all-to-all-start.2 = ((bf16[16,8,1280]{2,1,0:T(8,128)(2,1)}), bf16[16,8,1280]{2,1,0:T(8,128)(2,1)S(1)}, u32[]{:S(2)}, u32[]{:S(2)}) async-start(bf16[16,8,1280]{2,1,0:T(8,128)(2,1)} %bitcast.35), calls=%async_computation.2 | async-start | bytes 655360 | tf_op jit(solution)/shard_map/all_to_all | solution.py:328
  136.3 1.1 shard_map.69
  137.4 1.1 shard_map.68
  138.6 0.9 add_convert_fusion.12
  139.5 1.0 collective-permute-start.13
  140.9 5.0 %collective-permute-done.17 = bf16[128,512]{1,0:T(8,128)(2,1)S(1)} collective-permute-done((bf16[128,512]{1,0:T(8,128)(2,1)S(1)}, bf16[128,512]{1,0:T(8,128)(2,1)S(1)}, u32[]{:S(2)}, u32[]{:S(2)}) %collective-permute-start.17) | collective-permute-done | bytes 131104 | tf_op jit(solution)/shard_map/ppermute | solution.py:344
  146.0 2.2 %collective-permute-start.18 = (bf16[128,512]{1,0:T(8,128)(2,1)S(1)}, bf16[128,512]{1,0:T(8,128)(2,1)S(1)}, u32[]{:S(2)}, u32[]{:S(2)}) collective-permute-start(bf16[128,512]{1,0:T(8,128)(2,1)S(1)} %add_convert_fusion.8), channel_id=1, source_target_pairs={{32,0},{225,1},{64,32},{1,33},{96,64},{33,65},{128,96},{65,97},{16... | collective-permute-start | bytes 393224 | tf_op jit(solution)/shard_map/ppermute | solution.py:344
  148.4 1.2 collective-permute-start.22
  149.6 1.4 collective-permute-start.26
  151.1 3.4 %collective-permute-start.19 = (bf16[128,512]{1,0:T(8,128)(2,1)S(1)}, bf16[128,512]{1,0:T(8,128)(2,1)S(1)}, u32[]{:S(2)}, u32[]{:S(2)}) collective-permute-start(bf16[128,512]{1,0:T(8,128)(2,1)S(1)} %add_convert_fusion.7), channel_id=1, source_target_pairs={{32,0},{225,1},{64,32},{1,33},{96,64},{33,65},{128,96},{65,97},{16... | collective-permute-start | bytes 393224 | tf_op jit(solution)/shard_map/ppermute | solution.py:344
  154.5 1.4 collective-permute-start.15
  155.9 1.4 collective-permute-start.23
  157.3 1.4 collective-permute-start.27
  158.7 0.9 collective-permute-done.15.refs_0_
  159.6 1.4 collective-permute-done.23.refs_2_
  161.0 1.4 collective-permute-done.27.refs_3_
  162.4 1.0 shard_map.74
  163.5 1.5 collective-permute-done.28
  165.1 0.8 add_convert_fusion
  (59 shorter events, 1.9 us)
Async XLA Ops:
  0.0 3.8 %collective-permute-start = (bf16[128,1024]{1,0:T(8,128)(2,1)}, bf16[128,1024]{1,0:T(8,128)(2,1)S(1)}, u32[]{:S(2)}, u32[]{:S(2)}) collective-permute-start(bf16[128,1024]{1,0:T(8,128)(2,1)} %tok_ref.1), channel_id=1, source_target_pairs={{0,1},{1,0},{2,3},{3,2},{4,5},{5,4},{6,7},{7,6},{8,9},{9,8},{10,11... | collective-permute-start | bytes 786440 | tf_op jit(solution)/shard_map/ppermute | solution.py:280
  1.9 10.6 %collective-permute-start.1 = (bf16[136,1024]{1,0:T(8,128)(2,1)}, bf16[136,1024]{1,0:T(8,128)(2,1)S(1)}, u32[]{:S(2)}, u32[]{:S(2)}) collective-permute-start(bf16[136,1024]{1,0:T(8,128)(2,1)} %shard_map.64.refs_0_), channel_id=1, source_target_pairs={{0,32},{1,225},{32,64},{33,1},{64,96},{65,33},{96,128},{97,65},{12... | collective-permute-start | bytes 835592 | tf_op jit(solution)/shard_map/ppermute | solution.py:289
  3.8 11.5 %collective-permute-start.2 = (bf16[128,1024]{1,0:T(8,128)(2,1)S(1)}, bf16[128,1024]{1,0:T(8,128)(2,1)S(1)}, u32[]{:S(2)}, u32[]{:S(2)}) collective-permute-start(bf16[128,1024]{1,0:T(8,128)(2,1)S(1)} %collective-permute-done.refs_1_), channel_id=1, source_target_pairs={{0,32},{1,225},{32,64},{33,1},{64,96},{65,33},{96,128},{97,65},{12... | collective-permute-start | bytes 786440 | tf_op jit(solution)/shard_map/ppermute | solution.py:289
  12.5 7.8 %collective-permute-start.3 = (bf16[136,1024]{1,0:T(8,128)(2,1)S(1)}, bf16[136,1024]{1,0:T(8,128)(2,1)S(1)}, u32[]{:S(2)}, u32[]{:S(2)}) collective-permute-start(bf16[136,1024]{1,0:T(8,128)(2,1)S(1)} %collective-permute-done.1.refs_0_), channel_id=1, source_target_pairs={{0,32},{1,225},{32,64},{33,1},{64,96},{65,33},{96,128},{97,65},{12... | collective-permute-start | bytes 835592 | tf_op jit(solution)/shard_map/ppermute | solution.py:289
  15.3 7.8 %collective-permute-start.4 = (bf16[128,1024]{1,0:T(8,128)(2,1)S(1)}, bf16[128,1024]{1,0:T(8,128)(2,1)S(1)}, u32[]{:S(2)}, u32[]{:S(2)}) collective-permute-start(bf16[128,1024]{1,0:T(8,128)(2,1)S(1)} %collective-permute-done.2.refs_1_), channel_id=1, source_target_pairs={{0,32},{1,225},{32,64},{33,1},{64,96},{65,33},{96,128},{97,65},{12... | collective-permute-start | bytes 786440 | tf_op jit(solution)/shard_map/ppermute | solution.py:289
  20.2 12.7 %collective-permute-start.8 = (bf16[136,1024]{1,0:T(8,128)(2,1)S(1)}, bf16[136,1024]{1,0:T(8,128)(2,1)S(1)}, u32[]{:S(2)}, u32[]{:S(2)}) collective-permute-start(bf16[136,1024]{1,0:T(8,128)(2,1)S(1)} %collective-permute-done.3.refs_2_), channel_id=1, source_target_pairs={{0,32},{1,225},{32,64},{33,1},{64,96},{65,33},{96,128},{97,65},{12... | collective-permute-start | bytes 835592 | tf_op jit(solution)/shard_map/ppermute | solution.py:289
  23.1 10.0 %collective-permute-start.9 = (bf16[128,1024]{1,0:T(8,128)(2,1)S(1)}, bf16[128,1024]{1,0:T(8,128)(2,1)S(1)}, u32[]{:S(2)}, u32[]{:S(2)}) collective-permute-start(bf16[128,1024]{1,0:T(8,128)(2,1)S(1)} %collective-permute-done.4.refs_3_), channel_id=1, source_target_pairs={{0,32},{1,225},{32,64},{33,1},{64,96},{65,33},{96,128},{97,65},{12... | collective-permute-start | bytes 786440 | tf_op jit(solution)/shard_map/ppermute | solution.py:289
  23.1 1.0 copy-start
  24.1 29.8 %copy-start.3 = (s32[2]{0:T(128)}, s32[2]{0:T(128)S(1)}, u32[]{:S(2)}) copy-start(s32[2]{0:T(128)S(1)} %pad_add_fusion.scal_ref) | copy-start | bytes 28
  25.8 20.1 %all-to-all-start = ((bf16[16,8,1280]{2,1,0:T(8,128)(2,1)}), bf16[16,8,1280]{2,1,0:T(8,128)(2,1)}, u32[]{:S(2)}, u32[]{:S(2)}) async-start(bf16[16,8,1280]{2,1,0:T(8,128)(2,1)} %bitcast.4), calls=%async_computation | async-start | bytes 655360 | tf_op jit(solution)/shard_map/all_to_all | solution.py:305
  33.0 20.2 %copy-start.5 = (bf16[1,2048,384]{2,1,0:T(8,128)(2,1)S(1)}, bf16[1,2048,384]{2,1,0:T(8,128)(2,1)}, u32[]{:S(2)}) copy-start(bf16[1,2048,384]{2,1,0:T(8,128)(2,1)} %param.9) | copy-start | bytes 4718596
  33.0 7.8 %collective-permute-start.10 = (bf16[136,1024]{1,0:T(8,128)(2,1)S(1)}, bf16[136,1024]{1,0:T(8,128)(2,1)S(1)}, u32[]{:S(2)}, u32[]{:S(2)}) collective-permute-start(bf16[136,1024]{1,0:T(8,128)(2,1)S(1)} %collective-permute-done.8.refs_0_), channel_id=1, source_target_pairs={{0,32},{1,225},{32,64},{33,1},{64,96},{65,33},{96,128},{97,65},{12... | collective-permute-start | bytes 835592 | tf_op jit(solution)/shard_map/ppermute | solution.py:289
  33.1 10.5 %collective-permute-start.11 = (bf16[128,1024]{1,0:T(8,128)(2,1)S(1)}, bf16[128,1024]{1,0:T(8,128)(2,1)S(1)}, u32[]{:S(2)}, u32[]{:S(2)}) collective-permute-start(bf16[128,1024]{1,0:T(8,128)(2,1)S(1)} %collective-permute-done.9.refs_1_), channel_id=1, source_target_pairs={{0,32},{1,225},{32,64},{33,1},{64,96},{65,33},{96,128},{97,65},{12... | collective-permute-start | bytes 786440 | tf_op jit(solution)/shard_map/ppermute | solution.py:289
  46.0 20.2 %all-to-all-start.4 = ((bf16[16,8,3840]{2,1,0:T(8,128)(2,1)}), bf16[16,8,3840]{2,1,0:T(8,128)(2,1)}, u32[]{:S(2)}, u32[]{:S(2)}) async-start(bf16[16,8,3840]{2,1,0:T(8,128)(2,1)} %bitcast.15), calls=%async_computation.4 | async-start | bytes 1966080 | tf_op jit(solution)/shard_map/all_to_all | solution.py:305
  53.2 19.4 %collective-permute-start.5 = (bf16[2048,384]{1,0:T(8,128)(2,1)S(1)}, bf16[2048,384]{1,0:T(8,128)(2,1)}, u32[]{:S(2)}, u32[]{:S(2)}) collective-permute-start(bf16[2048,384]{1,0:T(8,128)(2,1)S(1)} %bitcast.26), channel_id=1, source_target_pairs={{0,1},{1,0},{2,3},{3,2},{4,5},{5,4},{6,7},{7,6},{8,9},{9,8},{10,11... | collective-permute-start | bytes 4718600 | tf_op jit(solution)/shard_map/ppermute | solution.py:292
  53.3 19.4 %collective-permute-start.6 = (bf16[2048,384]{1,0:T(8,128)(2,1)}, bf16[2048,384]{1,0:T(8,128)(2,1)}, u32[]{:S(2)}, u32[]{:S(2)}) collective-permute-start(bf16[2048,384]{1,0:T(8,128)(2,1)} %bitcast.27), channel_id=1, source_target_pairs={{0,1},{1,0},{2,3},{3,2},{4,5},{5,4},{6,7},{7,6},{8,9},{9,8},{10,11... | collective-permute-start | bytes 4718600 | tf_op jit(solution)/shard_map/ppermute | solution.py:292
  53.8 18.9 %collective-permute-start.7 = (bf16[384,2048]{1,0:T(8,128)(2,1)}, bf16[384,2048]{1,0:T(8,128)(2,1)}, u32[]{:S(2)}, u32[]{:S(2)}) collective-permute-start(bf16[384,2048]{1,0:T(8,128)(2,1)} %bitcast.30), channel_id=1, source_target_pairs={{0,1},{1,0},{2,3},{3,2},{4,5},{5,4},{6,7},{7,6},{8,9},{9,8},{10,11... | collective-permute-start | bytes 4718600 | tf_op jit(solution)/shard_map/ppermute | solution.py:292
  66.2 22.4 %all-to-all-start.1 = ((bf16[16,8,5120]{2,1,0:T(8,128)(2,1)}), bf16[16,8,5120]{2,1,0:T(8,128)(2,1)}, u32[]{:S(2)}, u32[]{:S(2)}) async-start(bf16[16,8,5120]{2,1,0:T(8,128)(2,1)} %bitcast.6), calls=%async_computation.1 | async-start | bytes 2621440 | tf_op jit(solution)/shard_map/all_to_all | solution.py:305
  88.6 18.9 %all-to-all-start.5 = ((bf16[16,8,3840]{2,1,0:T(8,128)(2,1)}), bf16[16,8,3840]{2,1,0:T(8,128)(2,1)S(1)}, u32[]{:S(2)}, u32[]{:S(2)}) async-start(bf16[16,8,3840]{2,1,0:T(8,128)(2,1)} %bitcast.33), calls=%async_computation.5 | async-start | bytes 1966080 | tf_op jit(solution)/shard_map/all_to_all | solution.py:328
  104.6 8.8 %copy-start.4 = (s32[2]{0:T(128)S(1)}, s32[2]{0:T(128)}, u32[]{:S(2)}) copy-start(s32[2]{0:T(128)} %copy-done.3) | copy-start | bytes 28
  107.4 22.7 %all-to-all-start.3 = ((bf16[16,8,5120]{2,1,0:T(8,128)(2,1)}), bf16[16,8,5120]{2,1,0:T(8,128)(2,1)S(1)}, u32[]{:S(2)}, u32[]{:S(2)}) async-start(bf16[16,8,5120]{2,1,0:T(8,128)(2,1)} %bitcast.34), calls=%async_computation.3 | async-start | bytes 2621440 | tf_op jit(solution)/shard_map/all_to_all | solution.py:328
  115.2 23.3 %collective-permute-start.12 = (bf16[128,512]{1,0:T(8,128)(2,1)}, bf16[128,512]{1,0:T(8,128)(2,1)}, u32[]{:S(2)}, u32[]{:S(2)}) collective-permute-start(bf16[128,512]{1,0:T(8,128)(2,1)} %get-tuple-element.52), channel_id=1, source_target_pairs={{32,0},{225,1},{64,32},{1,33},{96,64},{33,65},{128,96},{65,97},{16... | collective-permute-start | bytes 393224 | tf_op jit(solution)/shard_map/ppermute | solution.py:344
  117.3 0.7 copy-start.1
  118.0 22.5 %collective-permute-start.16 = (bf16[128,512]{1,0:T(8,128)(2,1)}, bf16[128,512]{1,0:T(8,128)(2,1)S(1)}, u32[]{:S(2)}, u32[]{:S(2)}) collective-permute-start(bf16[128,512]{1,0:T(8,128)(2,1)} %get-tuple-element.56), channel_id=1, source_target_pairs={{32,0},{225,1},{64,32},{1,33},{96,64},{33,65},{128,96},{65,97},{16... | collective-permute-start | bytes 393224 | tf_op jit(solution)/shard_map/ppermute | solution.py:344
  118.0 22.6 %collective-permute-start.20 = (bf16[128,512]{1,0:T(8,128)(2,1)}, bf16[128,512]{1,0:T(8,128)(2,1)S(1)}, u32[]{:S(2)}, u32[]{:S(2)}) collective-permute-start(bf16[128,512]{1,0:T(8,128)(2,1)} %get-tuple-element.60), channel_id=1, source_target_pairs={{32,0},{225,1},{64,32},{1,33},{96,64},{33,65},{128,96},{65,97},{16... | collective-permute-start | bytes 393224 | tf_op jit(solution)/shard_map/ppermute | solution.py:344
  118.1 22.7 %collective-permute-start.24 = (bf16[128,512]{1,0:T(8,128)(2,1)}, bf16[128,512]{1,0:T(8,128)(2,1)S(1)}, u32[]{:S(2)}, u32[]{:S(2)}) collective-permute-start(bf16[128,512]{1,0:T(8,128)(2,1)} %get-tuple-element.64), channel_id=1, source_target_pairs={{32,0},{225,1},{64,32},{1,33},{96,64},{33,65},{128,96},{65,97},{16... | collective-permute-start | bytes 393224 | tf_op jit(solution)/shard_map/ppermute | solution.py:344
  130.1 8.4 %copy-start.2 = (f32[128,512]{1,0:T(8,128)S(1)}, f32[128,512]{1,0:T(8,128)}, u32[]{:S(2)}) copy-start(f32[128,512]{1,0:T(8,128)} %copy-done.1) | copy-start | bytes 786436
  130.1 28.6 %all-to-all-start.2 = ((bf16[16,8,1280]{2,1,0:T(8,128)(2,1)}), bf16[16,8,1280]{2,1,0:T(8,128)(2,1)S(1)}, u32[]{:S(2)}, u32[]{:S(2)}) async-start(bf16[16,8,1280]{2,1,0:T(8,128)(2,1)} %bitcast.35), calls=%async_computation.2 | async-start | bytes 655360 | tf_op jit(solution)/shard_map/all_to_all | solution.py:328
  139.5 8.7 %collective-permute-start.13 = (bf16[128,512]{1,0:T(8,128)(2,1)S(1)}, bf16[128,512]{1,0:T(8,128)(2,1)S(1)}, u32[]{:S(2)}, u32[]{:S(2)}) collective-permute-start(bf16[128,512]{1,0:T(8,128)(2,1)S(1)} %add_convert_fusion.12), channel_id=1, source_target_pairs={{32,0},{225,1},{64,32},{1,33},{96,64},{33,65},{128,96},{65,97},{16... | collective-permute-start | bytes 393224 | tf_op jit(solution)/shard_map/ppermute | solution.py:344
  140.5 5.4 %collective-permute-start.17 = (bf16[128,512]{1,0:T(8,128)(2,1)S(1)}, bf16[128,512]{1,0:T(8,128)(2,1)S(1)}, u32[]{:S(2)}, u32[]{:S(2)}) collective-permute-start(bf16[128,512]{1,0:T(8,128)(2,1)S(1)} %add_convert_fusion.9), channel_id=1, source_target_pairs={{32,0},{225,1},{64,32},{1,33},{96,64},{33,65},{128,96},{65,97},{16... | collective-permute-start | bytes 393224 | tf_op jit(solution)/shard_map/ppermute | solution.py:344
  140.7 7.7 %collective-permute-start.21 = (bf16[128,512]{1,0:T(8,128)(2,1)S(1)}, bf16[128,512]{1,0:T(8,128)(2,1)S(1)}, u32[]{:S(2)}, u32[]{:S(2)}) collective-permute-start(bf16[128,512]{1,0:T(8,128)(2,1)S(1)} %add_convert_fusion.6), channel_id=1, source_target_pairs={{32,0},{225,1},{64,32},{1,33},{96,64},{33,65},{128,96},{65,97},{16... | collective-permute-start | bytes 393224 | tf_op jit(solution)/shard_map/ppermute | solution.py:344
  140.8 8.8 %collective-permute-start.25 = (bf16[128,512]{1,0:T(8,128)(2,1)S(1)}, bf16[128,512]{1,0:T(8,128)(2,1)S(1)}, u32[]{:S(2)}, u32[]{:S(2)}) collective-permute-start(bf16[128,512]{1,0:T(8,128)(2,1)S(1)} %add_convert_fusion.3), channel_id=1, source_target_pairs={{32,0},{225,1},{64,32},{1,33},{96,64},{33,65},{128,96},{65,97},{16... | collective-permute-start | bytes 393224 | tf_op jit(solution)/shard_map/ppermute | solution.py:344
  146.0 5.0 %collective-permute-start.18 = (bf16[128,512]{1,0:T(8,128)(2,1)S(1)}, bf16[128,512]{1,0:T(8,128)(2,1)S(1)}, u32[]{:S(2)}, u32[]{:S(2)}) collective-permute-start(bf16[128,512]{1,0:T(8,128)(2,1)S(1)} %add_convert_fusion.8), channel_id=1, source_target_pairs={{32,0},{225,1},{64,32},{1,33},{96,64},{33,65},{128,96},{65,97},{16... | collective-permute-start | bytes 393224 | tf_op jit(solution)/shard_map/ppermute | solution.py:344
  148.2 6.3 %collective-permute-start.14 = (bf16[128,512]{1,0:T(8,128)(2,1)S(1)}, bf16[128,512]{1,0:T(8,128)(2,1)S(1)}, u32[]{:S(2)}, u32[]{:S(2)}) collective-permute-start(bf16[128,512]{1,0:T(8,128)(2,1)S(1)} %add_convert_fusion.11), channel_id=1, source_target_pairs={{32,0},{225,1},{64,32},{1,33},{96,64},{33,65},{128,96},{65,97},{16... | collective-permute-start | bytes 393224 | tf_op jit(solution)/shard_map/ppermute | solution.py:344
  148.4 7.5 %collective-permute-start.22 = (bf16[128,512]{1,0:T(8,128)(2,1)S(1)}, bf16[128,512]{1,0:T(8,128)(2,1)S(1)}, u32[]{:S(2)}, u32[]{:S(2)}) collective-permute-start(bf16[128,512]{1,0:T(8,128)(2,1)S(1)} %add_convert_fusion.5), channel_id=1, source_target_pairs={{32,0},{225,1},{64,32},{1,33},{96,64},{33,65},{128,96},{65,97},{16... | collective-permute-start | bytes 393224 | tf_op jit(solution)/shard_map/ppermute | solution.py:344
  149.6 7.7 %collective-permute-start.26 = (bf16[128,512]{1,0:T(8,128)(2,1)S(1)}, bf16[128,512]{1,0:T(8,128)(2,1)S(1)}, u32[]{:S(2)}, u32[]{:S(2)}) collective-permute-start(bf16[128,512]{1,0:T(8,128)(2,1)S(1)} %add_convert_fusion.2), channel_id=1, source_target_pairs={{32,0},{225,1},{64,32},{1,33},{96,64},{33,65},{128,96},{65,97},{16... | collective-permute-start | bytes 393224 | tf_op jit(solution)/shard_map/ppermute | solution.py:344
  151.1 7.6 %collective-permute-start.19 = (bf16[128,512]{1,0:T(8,128)(2,1)S(1)}, bf16[128,512]{1,0:T(8,128)(2,1)S(1)}, u32[]{:S(2)}, u32[]{:S(2)}) collective-permute-start(bf16[128,512]{1,0:T(8,128)(2,1)S(1)} %add_convert_fusion.7), channel_id=1, source_target_pairs={{32,0},{225,1},{64,32},{1,33},{96,64},{33,65},{128,96},{65,97},{16... | collective-permute-start | bytes 393224 | tf_op jit(solution)/shard_map/ppermute | solution.py:344
  154.5 5.0 %collective-permute-start.15 = (bf16[128,512]{1,0:T(8,128)(2,1)S(1)}, bf16[128,512]{1,0:T(8,128)(2,1)S(1)}, u32[]{:S(2)}, u32[]{:S(2)}) collective-permute-start(bf16[128,512]{1,0:T(8,128)(2,1)S(1)} %add_convert_fusion.10), channel_id=1, source_target_pairs={{32,0},{225,1},{64,32},{1,33},{96,64},{33,65},{128,96},{65,97},{16... | collective-permute-start | bytes 393224 | tf_op jit(solution)/shard_map/ppermute | solution.py:344
  155.9 5.0 %collective-permute-start.23 = (bf16[128,512]{1,0:T(8,128)(2,1)S(1)}, bf16[128,512]{1,0:T(8,128)(2,1)S(1)}, u32[]{:S(2)}, u32[]{:S(2)}) collective-permute-start(bf16[128,512]{1,0:T(8,128)(2,1)S(1)} %add_convert_fusion.4), channel_id=1, source_target_pairs={{32,0},{225,1},{64,32},{1,33},{96,64},{33,65},{128,96},{65,97},{16... | collective-permute-start | bytes 393224 | tf_op jit(solution)/shard_map/ppermute | solution.py:344
  157.3 5.0 %collective-permute-start.27 = (bf16[128,512]{1,0:T(8,128)(2,1)S(1)}, bf16[128,512]{1,0:T(8,128)(2,1)S(1)}, u32[]{:S(2)}, u32[]{:S(2)}) collective-permute-start(bf16[128,512]{1,0:T(8,128)(2,1)S(1)} %add_convert_fusion.1), channel_id=1, source_target_pairs={{32,0},{225,1},{64,32},{1,33},{96,64},{33,65},{128,96},{65,97},{16... | collective-permute-start | bytes 393224 | tf_op jit(solution)/shard_map/ppermute | solution.py:344
  163.4 1.6 collective-permute-start.28
